TPU v7x, 32 devices: a whole 2x2x4 slice. The times are simulated.
32 devices in a mesh: gx: 4 (over y, x), gy: 8 (over z, core).
Axes of the slice: x: 2, y: 2, z: 4, core: 2. Of those that a mesh axis runs over, the one named last changes fastest.
Arguments:
- value_field: float32 [4, 24, 48, 1536], P(None, 'gx', 'gy'), may hold values from -16 to 17
- target_mask: int32 [4, 24, 48, 1536], P(None, 'gx', 'gy'), may hold values 0 or 1
- obstacle_mask: int32 [4, 24, 48, 1536], P(None, 'gx', 'gy'), may hold values 0 or 1
- drift_gains: float32 [5], replicated, may hold values from 0.5 to 2
- control_costs: float32 [5], replicated, may hold values from 0.25 to 1
Outputs:
- reach_value: float32 [4, 24, 48, 1536], P(None, 'gx', 'gy')
- time_steps: float32 [3], replicated
All inputs are finite; a program needn't handle non-finite values. No bound on the sum of `target_mask` or of `obstacle_mask` on one device may be relied on, other than what follows from the above.
Results may differ from a plain program's by a relative error of at most 0.0003.
Values sent between devices are 32-bit elements; how exact they have to be, the bound alone decides.
A program may use at most 128 MiB of HBM per device.

v0:
```python
import math

import jax
import jax.numpy as jnp
from jax import lax
from jax.sharding import PartitionSpec as P

N3 = 32
N4 = 48
GRID = 96
STEPS = 3


courant = 0.5
weno_eps = 1e-06


def with_halo(shard, sides, width):
    for axis, dim in sides:
        devices, length = (lax.axis_size(axis), shard.shape[dim])
        up = [(i, (i + 1) % devices) for i in range(devices)]
        down = [(j, i) for i, j in up]
        last = lax.slice_in_dim(shard, length - width, length, axis=dim)
        leading = lax.slice_in_dim(shard, 0, width, axis=dim)
        before = lax.ppermute(last, axis, up)
        after = lax.ppermute(leading, axis, down)
        shard = jnp.concatenate([before, shard, after], axis=dim)
    return shard


def weno_side(diff_one, diff_two, diff_three, diff_four, diff_five):
    stencil_one = diff_one / 3.0 - 7.0 * diff_two / 6.0 + 11.0 * diff_three / 6.0
    stencil_two = -diff_two / 6.0 + 5.0 * diff_three / 6.0 + diff_four / 3.0
    stencil_three = diff_three / 3.0 + 5.0 * diff_four / 6.0 - diff_five / 6.0
    smooth_one = (
        13.0 / 12.0 * (diff_one - 2.0 * diff_two + diff_three) ** 2
        + 0.25 * (diff_one - 4.0 * diff_two + 3.0 * diff_three) ** 2
    )
    smooth_two = (
        13.0 / 12.0 * (diff_two - 2.0 * diff_three + diff_four) ** 2
        + 0.25 * (diff_two - diff_four) ** 2
    )
    smooth_three = (
        13.0 / 12.0 * (diff_three - 2.0 * diff_four + diff_five) ** 2
        + 0.25 * (3.0 * diff_three - 4.0 * diff_four + diff_five) ** 2
    )
    weight_one = 0.1 / (weno_eps + smooth_one) ** 2
    weight_two = 0.6 / (weno_eps + smooth_two) ** 2
    weight_three = 0.3 / (weno_eps + smooth_three) ** 2
    return (weight_one * stencil_one + weight_two * stencil_two + weight_three * stencil_three) / (
        weight_one + weight_two + weight_three
    )


def axis_slopes(shifted, spacing):
    differences = [shifted[offset + 1] - shifted[offset] for offset in range(6)]
    minus_slope = (
        weno_side(differences[0], differences[1], differences[2], differences[3], differences[4])
        / spacing
    )
    plus_slope = (
        weno_side(differences[5], differences[4], differences[3], differences[2], differences[1])
        / spacing
    )
    return (minus_slope, plus_slope)


def merged_shifts(interior, stride, position, extent):
    upward = []
    current = interior
    for offset in range(1, 4):
        current = jnp.where(
            position + offset <= extent - 1, jnp.roll(interior, -offset * stride, axis=-1), current
        )
        upward.append(current)
    downward = []
    current = interior
    for offset in range(1, 4):
        current = jnp.where(
            position - offset >= 0, jnp.roll(interior, offset * stride, axis=-1), current
        )
        downward.append(current)
    return [downward[2], downward[1], downward[0], interior, upward[0], upward[1], upward[2]]


def along_unsplit(interior, spacing_list):
    plane_count = interior.shape[0]
    padded = jnp.pad(interior, ((3, 3), (0, 0), (0, 0), (0, 0)), mode="edge")
    neighbours = [padded[offset : offset + plane_count] for offset in range(7)]
    lane_index = jnp.arange(interior.shape[3], dtype=jnp.int32)
    return [
        axis_slopes(neighbours, spacing_list[0]),
        axis_slopes(merged_shifts(interior, N4, lane_index // N4, N3), spacing_list[3]),
        axis_slopes(merged_shifts(interior, 1, lane_index % N4, N4), spacing_list[4]),
    ]


def finish(
    extended,
    along_axes,
    margin,
    target_part,
    obstacle_part,
    drift_gains,
    control_costs,
    spacing_list,
):
    plane_count = extended.shape[0]
    rows_out = extended.shape[1] - 6
    cols_out = extended.shape[2] - 6
    owned_rows = rows_out - 2 * margin
    owned_cols = cols_out - 2 * margin
    interior = extended[:, 3 : 3 + rows_out, 3 : 3 + cols_out]
    row_slopes = axis_slopes(
        [extended[:, offset : offset + rows_out, 3 : 3 + cols_out] for offset in range(7)],
        spacing_list[1],
    )
    col_slopes = axis_slopes(
        [extended[:, 3 : 3 + rows_out, offset : offset + cols_out] for offset in range(7)],
        spacing_list[2],
    )
    slopes = [along_axes[0], row_slopes, col_slopes, along_axes[1], along_axes[2]]
    first_row = lax.axis_index("gx") * owned_rows - margin
    first_col = lax.axis_index("gy") * owned_cols - margin
    first_pos = (
        (jnp.arange(plane_count, dtype=jnp.float32) - plane_count / 2 + 0.5) * (2.0 / GRID)
    ).reshape(plane_count, 1, 1, 1)
    heading_one = (
        2.0
        * math.pi
        / (owned_rows * lax.axis_size("gx"))
        * (first_row + jnp.arange(rows_out, dtype=jnp.int32)).astype(jnp.float32)
    ).reshape(1, rows_out, 1, 1)
    heading_two = (
        2.0
        * math.pi
        / (owned_cols * lax.axis_size("gy"))
        * (first_col + jnp.arange(cols_out, dtype=jnp.int32)).astype(jnp.float32)
    ).reshape(1, 1, cols_out, 1)
    lane_index = jnp.arange(extended.shape[3], dtype=jnp.int32)
    third_pos = (((lane_index // N4).astype(jnp.float32) - N3 / 2 + 0.5) * (2.0 / GRID)).reshape(
        1, 1, 1, -1
    )
    fourth_pos = (((lane_index % N4).astype(jnp.float32) - N4 / 2 + 0.5) * (2.0 / GRID)).reshape(
        1, 1, 1, -1
    )
    drift_terms = [
        drift_gains[0] * (jnp.cos(heading_one) - 0.5 * jnp.cos(heading_two) + third_pos),
        drift_gains[1] * (fourth_pos - 0.3 * first_pos),
        drift_gains[2] * (third_pos + 0.5 * jnp.sin(heading_one)),
        drift_gains[3] * (jnp.sin(heading_two) - first_pos),
        drift_gains[4] * (jnp.cos(heading_one) * jnp.sin(heading_two) - fourth_pos),
    ]
    peaks = []
    for axis_number in range(5):
        scale = control_costs[axis_number] * spacing_list[axis_number]
        speed = jnp.maximum(
            jnp.abs(drift_terms[axis_number] - scale * slopes[axis_number][0]),
            jnp.abs(drift_terms[axis_number] - scale * slopes[axis_number][1]),
        )
        peaks.append(jnp.max(speed))
    bounds = lax.pmax(jnp.stack(peaks), ("gx", "gy"))
    spacing_array = jnp.array(spacing_list, dtype=jnp.float32)
    time_step = courant / (jnp.sum(bounds / spacing_array) + 1e-06)
    hamiltonian = jnp.zeros_like(interior)
    for axis_number in range(5):
        minus_slope, plus_slope = slopes[axis_number]
        middle = 0.5 * (minus_slope + plus_slope)
        hamiltonian = (
            hamiltonian
            + drift_terms[axis_number] * middle
            - 0.5 * control_costs[axis_number] * spacing_list[axis_number] * middle * middle
        )
        hamiltonian = hamiltonian - bounds[axis_number] * 0.5 * (plus_slope - minus_slope)
    advanced = interior - time_step * hamiltonian
    advanced = jnp.where(target_part == 1, jnp.minimum(advanced, -0.5), advanced)
    advanced = jnp.where(obstacle_part == 1, jnp.maximum(advanced, 0.5), advanced)
    return (advanced, time_step)


def thin_step(value_now, target_mask, obstacle_mask, drift_gains, control_costs, spacing_list):
    along_axes = None
    extended = with_halo(value_now, (("gx", 1), ("gy", 2)), 3)
    along_axes = along_unsplit(extended[:, 3:-3, 3:-3], spacing_list)
    return finish(
        extended,
        along_axes,
        0,
        target_mask,
        obstacle_mask,
        drift_gains,
        control_costs,
        spacing_list,
    )


def body(value_field, target_mask, obstacle_mask, drift_gains, control_costs):
    spacing_list = [
        2.0 / GRID,
        2.0 * math.pi / (value_field.shape[1] * lax.axis_size("gx")),
        2.0 * math.pi / (value_field.shape[2] * lax.axis_size("gy")),
        2.0 / GRID,
        2.0 / GRID,
    ]
    value_now = value_field
    step_sizes = []
    remaining = STEPS
    for section_number in range(remaining):
        value_now, time_step = thin_step(
            value_now, target_mask, obstacle_mask, drift_gains, control_costs, spacing_list
        )
        step_sizes.append(time_step)
    return (value_now, jnp.stack(step_sizes))


def solution(mesh):
    return jax.shard_map(
        body,
        mesh=mesh,
        in_specs=(
            P(None, "gx", "gy", None),
            P(None, "gx", "gy", None),
            P(None, "gx", "gy", None),
            P(),
            P(),
        ),
        out_specs=(P(None, "gx", "gy", None), P()),
        check_vma=False,
    )
```

profile of v0, /device:TPU:0, one launch (start us, length us, event | category | flops | bytes accessed | tf_op | source)
XLA Modules:
  0.0 385.3 jit_solution(1386984626563395664)
XLA Ops:
  20.0 5.7 %collective-permute-done.1 = f32[4,3,6,1536]{3,0,2,1:T(4,128)S(1)} collective-permute-done((f32[4,3,6,1536]{3,0,2,1:T(4,128)S(1)}, f32[4,3,6,1536]{3,0,2,1:T(4,128)S(1)}, u32[]{:S(2)}, u32[]{:S(2)}) %collective-permute-start.1) | collective-permute-done | bytes 442400 | tf_op jit(solution)/shard_map/ppermute | solution.py:26
  25.9 7.8 %maximum_reduce_fusion.13 = (f32[]{:T(128)}, f32[4,6,6,1536]{3,2,1,0:T(8,128)S(1)}, f32[4,6,6,1536]{3,2,1,0:T(8,128)}, f32[4,6,6,1536]{3,2,1,0:T(8,128)S(1)}) fusion(f32[]{:T(128)} %bitcast.6, f32[4,1536]{1,0:T(4,128)S(1)} %get-tuple-element.157, f32[4,9,6,1536]{3,2,1,0:T(8,128)S(1)} %get-tuple-element.150, f32[4,6,6,1536]{3,0,2,1:T(4,128)S(1)} %copy-done, ...), kind=kLoop, calls=%fused_computation.260 | loop fusion | flops 30523392 | bytes 8871944 | tf_op jit(solution)/shard_map/reduce_max | solution.py:161
  42.3 8.0 %maximum_reduce_fusion.14 = (f32[]{:T(128)}, f32[4,6,6,1536]{3,2,1,0:T(8,128)}, f32[4,6,6,1536]{3,2,1,0:T(8,128)}) fusion(f32[]{:T(128)} %bitcast.3, f32[6,6,1536]{2,1,0:T(8,128)S(1)} %copy-done.1, f32[3,6,6,1536]{3,2,1,0:T(8,128)S(1)} %reshape.295, f32[4,6,6,1536]{3,2,1,0:T(8,128)S(1)} %get-tuple-element.142, f32[4,6,6,1536]{3,0,2,1:T(4,128)S(1)} %copy-done, ...), kind=kLoop, calls=%fused_computation.263 | loop fusion | flops 33841152 | bytes 5087240 | tf_op jit(solution)/shard_map/reduce_max | solution.py:161
  50.4 10.5 %maximum_reduce_fusion.10 = (f32[]{:T(128)}, f32[4,6,6,1536]{3,2,1,0:T(8,128)}, f32[4,6,6,1536]{3,2,1,0:T(8,128)}) fusion(f32[]{:T(128)} %bitcast.15, f32[6,6,1536]{2,1,0:T(8,128)S(1)} %get-tuple-element.155, f32[4,6,6,2]{3,2,1,0:T(8,128)S(1)} %get-tuple-element.135, f32[4,6,6,1534]{3,2,1,0:T(8,128)S(1)} %get-tuple-element.137, ...), kind=kLoop, calls=%fused_computation.246 | loop fusion | flops 33177600 | bytes 8193032 | tf_op jit(solution)/shard_map/reduce_max | solution.py:161
  60.9 9.4 %maximum_reduce_fusion.11 = (f32[]{:T(128)}, f32[4,6,6,1536]{3,2,1,0:T(8,128)}, f32[4,6,6,1536]{3,2,1,0:T(8,128)}) fusion(f32[]{:T(128)} %bitcast.12, f32[4,6]{1,0:T(4,128)S(1)} %copy-done.39, f32[4,6,6,96]{3,2,1,0:T(8,128)S(1)} %get-tuple-element.123, f32[4,6,6,1440]{3,2,1,0:T(8,128)S(1)} %get-tuple-element.125, pred[1536]{0:T(1024)(128)(4,1)S(1)} %copy-done.24, ...), kind=kLoop, calls=%fused_computation.249 | loop fusion | flops 33177600 | bytes 7971944 | tf_op jit(solution)/shard_map/reduce_max | solution.py:161
  71.5 9.1 %maximum_reduce_fusion.12 = (f32[]{:T(128)}, f32[4,6,6,1536]{3,2,1,0:T(8,128)}, f32[4,6,6,1536]{3,2,1,0:T(8,128)}) fusion(f32[]{:T(128)} %bitcast.9, f32[6,1536]{1,0:T(8,128)S(1)} %copy-done.9, f32[4,12,3,1536]{3,2,1,0:T(4,128)S(1)} %copy.82, f32[4,12,6,1536]{3,2,1,0:T(8,128)S(1)} %get-tuple-element.151, f32[4,6,6,1536]{3,0,2,1:T(4,128)S(1)} %copy-done, ...), kind=kLoop, calls=%fused_computation.252 | loop fusion | flops 31850496 | bytes 6230024 | tf_op jit(solution)/shard_map/reduce_max | solution.py:161
  84.6 38.9 %pmax.21 = f32[5]{0:T(128)S(1)} all-reduce(f32[5]{0:T(128)S(1)} %stack.71), channel_id=1, replica_groups=mesh['gx'=4,'gy'=8] {'gx','gy'}, use_global_device_ids=true, to_apply=%region_5.6 | all-reduce | flops 5 | bytes 40 | tf_op jit(solution)/shard_map/pmax | solution.py:162
  129.2 7.1 %maximum_select_fusion.2 = (f32[4,6,6,1536]{3,2,1,0:T(8,128)S(1)}, pred[4,6,6,1536]{3,2,1,0:T(8,128)(4,1)}, pred[4,6,6,1536]{3,2,1,0:T(8,128)(4,1)}) fusion(f32[4,6,6,1536]{3,0,2,1:T(4,128)S(1)} %copy-done, f32[4,6,6,1536]{3,2,1,0:T(8,128)} %get-tuple-element.41, f32[4,6,6,1536]{3,2,1,0:T(8,128)} %get-tuple-element.40, ...), kind=kLoop, calls=%fused_computation.54 | loop fusion | flops 14819328 | bytes 13332620 | tf_op jit(solution)/shard_map/jit(_where)/select_n | solution.py:177
  143.8 7.9 %maximum_reduce_fusion.9 = (f32[]{:T(128)}, f32[4,6,6,1536]{3,2,1,0:T(8,128)}, f32[4,6,6,1536]{3,2,1,0:T(8,128)}) fusion(f32[]{:T(128)} %bitcast.3, f32[6,6,1536]{2,1,0:T(8,128)S(1)} %copy-done.2, f32[4,6,6,1536]{3,2,1,0:T(8,128)S(1)} %get-tuple-element.36, f32[3,6,6,1536]{3,2,1,0:T(8,128)S(1)} %reshape.297, f32[3,6,6,1536]{3,2,1,0:T(8,128)S(1)} %reshape.296), kind=kLoop, calls=%fused_computation.234 | loop fusion | flops 33841152 | bytes 4202504 | tf_op jit(solution)/shard_map/reduce_max | solution.py:161
  151.8 10.2 %maximum_reduce_fusion.5 = (f32[]{:T(128)}, f32[4,6,6,1536]{3,2,1,0:T(8,128)}, f32[4,6,6,1536]{3,2,1,0:T(8,128)}) fusion(f32[]{:T(128)} %bitcast.15, f32[6,6,1536]{2,1,0:T(8,128)S(1)} %get-tuple-element.155, f32[4,6,6,2]{3,2,1,0:T(8,128)S(1)} %get-tuple-element.109, f32[4,6,6,1534]{3,2,1,0:T(8,128)S(1)} %get-tuple-element.111, ...), kind=kLoop, calls=%fused_computation.221 | loop fusion | flops 33177600 | bytes 8193032 | tf_op jit(solution)/shard_map/reduce_max | solution.py:161
  162.1 9.3 %maximum_reduce_fusion.6 = (f32[]{:T(128)}, f32[4,6,6,1536]{3,2,1,0:T(8,128)}, f32[4,6,6,1536]{3,2,1,0:T(8,128)}) fusion(f32[]{:T(128)} %bitcast.12, f32[4,6]{1,0:T(4,128)S(1)} %copy-done.40, f32[4,6,6,96]{3,2,1,0:T(8,128)S(1)} %get-tuple-element.97, f32[4,6,6,1440]{3,2,1,0:T(8,128)S(1)} %get-tuple-element.99, pred[1536]{0:T(1024)(128)(4,1)S(1)} %copy-done.25, ...), kind=kLoop, calls=%fused_computation.224 | loop fusion | flops 33177600 | bytes 7971944 | tf_op jit(solution)/shard_map/reduce_max | solution.py:161
  174.3 8.0 %maximum_reduce_fusion.8 = (f32[]{:T(128)}, f32[4,6,6,1536]{3,2,1,0:T(8,128)}, f32[4,6,6,1536]{3,2,1,0:T(8,128)}) fusion(f32[]{:T(128)} %bitcast.6, f32[4,1536]{1,0:T(4,128)S(1)} %copy-done.13, f32[4,6,6,1536]{3,2,1,0:T(8,128)S(1)} %get-tuple-element.36, f32[4,3,6,1536]{3,2,1,0:T(8,128)S(1)} %copy.120, f32[4,3,6,1536]{3,2,1,0:T(8,128)S(1)} %copy.118), kind=kLoop, calls=%fused_computation.231 | loop fusion | flops 33841152 | bytes 3563528 | tf_op jit(solution)/shard_map/reduce_max | solution.py:161
  182.3 9.3 %collective-permute-done.7 = f32[4,12,3,1536]{3,0,2,1:T(4,128)S(1)} collective-permute-done((f32[4,12,3,1536]{3,0,2,1:T(4,128)S(1)}, f32[4,12,3,1536]{3,0,2,1:T(4,128)S(1)}, u32[]{:S(2)}, u32[]{:S(2)}) %collective-permute-start.7) | collective-permute-done | bytes 884768 | tf_op jit(solution)/shard_map/ppermute | solution.py:26
  196.9 9.1 %maximum_reduce_fusion.7 = (f32[]{:T(128)}, f32[4,6,6,1536]{3,2,1,0:T(8,128)}, f32[4,6,6,1536]{3,2,1,0:T(8,128)}) fusion(f32[]{:T(128)} %bitcast.9, f32[6,1536]{1,0:T(8,128)S(1)} %copy-done.10, f32[4,12,3,1536]{3,2,1,0:T(4,128)S(1)} %copy.126, f32[4,3,6,1536]{3,2,1,0:T(8,128)S(1)} %copy.120, f32[4,6,6,1536]{3,2,1,0:T(8,128)S(1)} %get-tuple-element.36, ...), kind=kLoop, calls=%fused_computation.227 | loop fusion | flops 34504704 | bytes 5345288 | tf_op jit(solution)/shard_map/reduce_max | solution.py:161
  209.4 40.1 %pmax.22 = f32[5]{0:T(128)S(1)} all-reduce(f32[5]{0:T(128)S(1)} %stack.77), channel_id=1, replica_groups=mesh['gx'=4,'gy'=8] {'gx','gy'}, use_global_device_ids=true, to_apply=%region_12.13 | all-reduce | flops 5 | bytes 40 | tf_op jit(solution)/shard_map/pmax | solution.py:162
  254.9 6.2 %maximum_select_fusion.1 = f32[4,6,6,1536]{3,2,1,0:T(8,128)S(1)} fusion(pred[4,6,6,1536]{3,2,1,0:T(8,128)(4,1)} %get-tuple-element.38, pred[4,6,6,1536]{3,2,1,0:T(8,128)(4,1)S(1)} %copy-done.8, f32[4,6,6,1536]{3,2,1,0:T(8,128)S(1)} %get-tuple-element.36, f32[4,6,6,1536]{3,2,1,0:T(8,128)} %get-tuple-element.23, f32[4,6,6,1536]{3,2,1,0:T(8,128)} %get-tuple-element.22, ...), kind=kLoop, calls=%fused_computation.48 | loop fusion | flops 14376960 | bytes 11563148 | tf_op jit(solution)/shard_map/jit(_where)/select_n | solution.py:177
  268.3 7.8 %maximum_reduce_fusion.4 = (f32[]{:T(128)}, f32[4,6,6,1536]{3,2,1,0:T(8,128)}, f32[4,6,6,1536]{3,2,1,0:T(8,128)}) fusion(f32[]{:T(128)} %bitcast.3, f32[6,6,1536]{2,1,0:T(8,128)S(1)} %copy-done.3, f32[4,6,6,1536]{3,2,1,0:T(8,128)S(1)} %maximum_select_fusion.1, f32[3,6,6,1536]{3,2,1,0:T(8,128)S(1)} %reshape.299, f32[3,6,6,1536]{3,2,1,0:T(8,128)S(1)} %reshape.298), kind=kLoop, calls=%fused_computation.209 | loop fusion | flops 33841152 | bytes 4202504 | tf_op jit(solution)/shard_map/reduce_max | solution.py:161
  276.2 10.2 %maximum_reduce_fusion = (f32[]{:T(128)}, f32[4,6,6,1536]{3,2,1,0:T(8,128)}, f32[4,6,6,1536]{3,2,1,0:T(8,128)}) fusion(f32[]{:T(128)} %bitcast.15, f32[6,6,1536]{2,1,0:T(8,128)S(1)} %get-tuple-element.155, f32[4,6,6,2]{3,2,1,0:T(8,128)S(1)} %get-tuple-element.81, f32[4,6,6,1534]{3,2,1,0:T(8,128)S(1)} %get-tuple-element.83, ...), kind=kLoop, calls=%fused_computation.196 | loop fusion | flops 33177600 | bytes 8193032 | tf_op jit(solution)/shard_map/reduce_max | solution.py:161
  286.5 9.3 %maximum_reduce_fusion.1 = (f32[]{:T(128)}, f32[4,6,6,1536]{3,2,1,0:T(8,128)}, f32[4,6,6,1536]{3,2,1,0:T(8,128)}) fusion(f32[]{:T(128)} %bitcast.12, f32[4,6]{1,0:T(4,128)S(1)} %copy-done.41, f32[4,6,6,96]{3,2,1,0:T(8,128)S(1)} %get-tuple-element.69, f32[4,6,6,1440]{3,2,1,0:T(8,128)S(1)} %get-tuple-element.71, pred[1536]{0:T(1024)(128)(4,1)S(1)} %copy-done.26, ...), kind=kLoop, calls=%fused_computation.199 | loop fusion | flops 33177600 | bytes 7971944 | tf_op jit(solution)/shard_map/reduce_max | solution.py:161
  298.6 7.9 %maximum_reduce_fusion.3 = (f32[]{:T(128)}, f32[4,6,6,1536]{3,2,1,0:T(8,128)}, f32[4,6,6,1536]{3,2,1,0:T(8,128)}) fusion(f32[]{:T(128)} %bitcast.6, f32[4,1536]{1,0:T(4,128)S(1)} %copy-done.14, f32[4,6,6,1536]{3,2,1,0:T(8,128)S(1)} %maximum_select_fusion.1, f32[4,3,6,1536]{3,2,1,0:T(8,128)S(1)} %copy.130, f32[4,3,6,1536]{3,2,1,0:T(8,128)S(1)} %copy.128), kind=kLoop, calls=%fused_computation.206 | loop fusion | flops 33841152 | bytes 3563528 | tf_op jit(solution)/shard_map/reduce_max | solution.py:161
  306.5 9.4 %collective-permute-done.11 = f32[4,12,3,1536]{3,0,2,1:T(4,128)S(1)} collective-permute-done((f32[4,12,3,1536]{3,0,2,1:T(4,128)S(1)}, f32[4,12,3,1536]{3,0,2,1:T(4,128)S(1)}, u32[]{:S(2)}, u32[]{:S(2)}) %collective-permute-start.11) | collective-permute-done | bytes 884768 | tf_op jit(solution)/shard_map/ppermute | solution.py:26
  320.5 9.2 %maximum_reduce_fusion.2 = (f32[]{:T(128)}, f32[4,6,6,1536]{3,2,1,0:T(8,128)}, f32[4,6,6,1536]{3,2,1,0:T(8,128)}) fusion(f32[]{:T(128)} %bitcast.9, f32[6,1536]{1,0:T(8,128)S(1)} %copy-done.11, f32[4,12,3,1536]{3,2,1,0:T(4,128)S(1)} %copy.136, f32[4,3,6,1536]{3,2,1,0:T(8,128)S(1)} %copy.130, f32[4,6,6,1536]{3,2,1,0:T(8,128)S(1)} %maximum_select_fusion.1, ...), kind=kLoop, calls=%fused_computation.202 | loop fusion | flops 34504704 | bytes 5345288 | tf_op jit(solution)/shard_map/reduce_max | solution.py:161
  332.9 39.3 %pmax.23 = f32[5]{0:T(128)S(1)} all-reduce(f32[5]{0:T(128)S(1)} %stack.83), channel_id=1, replica_groups=mesh['gx'=4,'gy'=8] {'gx','gy'}, use_global_device_ids=true, to_apply=%region_19.20 | all-reduce | flops 5 | bytes 40 | tf_op jit(solution)/shard_map/pmax | solution.py:162
  377.5 5.5 %maximum_select_fusion = f32[4,6,6,1536]{3,2,1,0:T(8,128)S(1)} fusion(pred[4,6,6,1536]{3,2,1,0:T(8,128)(4,1)} %get-tuple-element.38, pred[4,6,6,1536]{3,2,1,0:T(8,128)(4,1)} %get-tuple-element.37, f32[4,6,6,1536]{3,2,1,0:T(8,128)S(1)} %maximum_select_fusion.1, f32[4,6,6,1536]{3,2,1,0:T(8,128)S(1)} %copy-done.5, f32[4,6,6,1536]{3,2,1,0:T(8,128)S(1)} %copy-done.4, ...), kind=kLoop, calls=%fused_computation.42 | loop fusion | flops 14376960 | bytes 11563148 | tf_op jit(solution)/shard_map/jit(_where)/select_n | solution.py:177
  (222 shorter events, 73.0 us)
Async XLA Ops:
  1.9 17.6 %collective-permute-start = (f32[4,3,6,1536]{3,0,2,1:T(4,128)S(1)}, f32[4,3,6,1536]{3,0,2,1:T(4,128)S(1)}, u32[]{:S(2)}, u32[]{:S(2)}) collective-permute-start(f32[4,3,6,1536]{3,0,2,1:T(4,128)S(1)} %get-tuple-element.147), channel_id=1, source_target_pairs={{0,8},{8,16},{16,24},{24,0},{1,9},{9,17},{17,25},{25,1},{2,10},{10... | collective-permute-start | bytes 1327112 | tf_op jit(solution)/shard_map/ppermute | solution.py:25
  4.9 20.9 %collective-permute-start.1 = (f32[4,3,6,1536]{3,0,2,1:T(4,128)S(1)}, f32[4,3,6,1536]{3,0,2,1:T(4,128)S(1)}, u32[]{:S(2)}, u32[]{:S(2)}) collective-permute-start(f32[4,3,6,1536]{3,0,2,1:T(4,128)S(1)} %get-tuple-element.146), channel_id=1, source_target_pairs={{8,0},{16,8},{24,16},{0,24},{9,1},{17,9},{25,17},{1,25},{10,2},{18... | collective-permute-start | bytes 1327112 | tf_op jit(solution)/shard_map/ppermute | solution.py:26
  37.9 32.4 %collective-permute-start.3 = (f32[4,12,3,1536]{3,0,2,1:T(4,128)S(1)}, f32[4,12,3,1536]{3,0,2,1:T(4,128)S(1)}, u32[]{:S(2)}, u32[]{:S(2)}) collective-permute-start(f32[4,12,3,1536]{3,0,2,1:T(4,128)S(1)} %copy.81), channel_id=1, source_target_pairs={{1,0},{2,1},{3,2},{4,3},{5,4},{6,5},{7,6},{0,7},{9,8},{10,9},{11,1... | collective-permute-start | bytes 2654216 | tf_op jit(solution)/shard_map/ppermute | solution.py:26
  40.7 30.0 %collective-permute-start.2 = (f32[4,12,3,1536]{3,0,2,1:T(4,128)S(1)}, f32[4,12,3,1536]{3,0,2,1:T(4,128)S(1)}, u32[]{:S(2)}, u32[]{:S(2)}) collective-permute-start(f32[4,12,3,1536]{3,0,2,1:T(4,128)S(1)} %copy.78), channel_id=1, source_target_pairs={{0,1},{1,2},{2,3},{3,4},{4,5},{5,6},{6,7},{7,0},{8,9},{9,10},{10,1... | collective-permute-start | bytes 2654216 | tf_op jit(solution)/shard_map/ppermute | solution.py:25
  50.3 10.5 %copy-start.21 = (pred[1536]{0:T(1024)(128)(4,1)S(1)}, pred[1536]{0:T(1024)(128)(4,1)}, u32[]{:S(2)}) copy-start(pred[1536]{0:T(1024)(128)(4,1)} %get-tuple-element.193) | copy-start | bytes 4612
  50.3 10.5 %copy-start.24 = (pred[1536]{0:T(1024)(128)(4,1)S(1)}, pred[1536]{0:T(1024)(128)(4,1)}, u32[]{:S(2)}) copy-start(pred[1536]{0:T(1024)(128)(4,1)} %get-tuple-element.194) | copy-start | bytes 4612
  50.3 10.5 %copy-start.27 = (pred[1536]{0:T(1024)(128)(4,1)S(1)}, pred[1536]{0:T(1024)(128)(4,1)}, u32[]{:S(2)}) copy-start(pred[1536]{0:T(1024)(128)(4,1)} %get-tuple-element.195) | copy-start | bytes 4612
  50.3 10.5 %copy-start.30 = (pred[1536]{0:T(1024)(128)(4,1)S(1)}, pred[1536]{0:T(1024)(128)(4,1)}, u32[]{:S(2)}) copy-start(pred[1536]{0:T(1024)(128)(4,1)} %get-tuple-element.196) | copy-start | bytes 4612
  139.9 31.5 %collective-permute-start.5 = (f32[4,3,6,1536]{3,0,2,1:T(4,128)S(1)}, f32[4,3,6,1536]{3,0,2,1:T(4,128)S(1)}, u32[]{:S(2)}, u32[]{:S(2)}) collective-permute-start(f32[4,3,6,1536]{3,0,2,1:T(4,128)S(1)} %copy.119), channel_id=1, source_target_pairs={{8,0},{16,8},{24,16},{0,24},{9,1},{17,9},{25,17},{1,25},{10,2},{18... | collective-permute-start | bytes 1327112 | tf_op jit(solution)/shard_map/ppermute | solution.py:26
  142.6 29.0 %collective-permute-start.4 = (f32[4,3,6,1536]{3,0,2,1:T(4,128)S(1)}, f32[4,3,6,1536]{3,0,2,1:T(4,128)S(1)}, u32[]{:S(2)}, u32[]{:S(2)}) collective-permute-start(f32[4,3,6,1536]{3,0,2,1:T(4,128)S(1)} %copy.117), channel_id=1, source_target_pairs={{0,8},{8,16},{16,24},{24,0},{1,9},{9,17},{17,25},{25,1},{2,10},{10... | collective-permute-start | bytes 1327112 | tf_op jit(solution)/shard_map/ppermute | solution.py:25
  173.1 18.5 %collective-permute-start.7 = (f32[4,12,3,1536]{3,0,2,1:T(4,128)S(1)}, f32[4,12,3,1536]{3,0,2,1:T(4,128)S(1)}, u32[]{:S(2)}, u32[]{:S(2)}) collective-permute-start(f32[4,12,3,1536]{3,0,2,1:T(4,128)S(1)} %copy.125), channel_id=1, source_target_pairs={{1,0},{2,1},{3,2},{4,3},{5,4},{6,5},{7,6},{0,7},{9,8},{10,9},{11,1... | collective-permute-start | bytes 2654216 | tf_op jit(solution)/shard_map/ppermute | solution.py:26
  174.0 22.4 %collective-permute-start.6 = (f32[4,12,3,1536]{3,0,2,1:T(4,128)S(1)}, f32[4,12,3,1536]{3,0,2,1:T(4,128)S(1)}, u32[]{:S(2)}, u32[]{:S(2)}) collective-permute-start(f32[4,12,3,1536]{3,0,2,1:T(4,128)S(1)} %copy.123), channel_id=1, source_target_pairs={{0,1},{1,2},{2,3},{3,4},{4,5},{5,6},{6,7},{7,0},{8,9},{9,10},{10,1... | collective-permute-start | bytes 2654216 | tf_op jit(solution)/shard_map/ppermute | solution.py:25
  196.9 53.4 %copy-start.45 = (f32[5]{0:T(128)S(1)}, f32[5]{0:T(128)}, u32[]{:S(2)}) copy-start(f32[5]{0:T(128)} %constant.541) | copy-start | bytes 64
  196.9 58.0 %copy-start.6 = (f32[6,6,1536]{2,1,0:T(8,128)S(1)}, f32[6,6,1536]{2,1,0:T(8,128)}, u32[]{:S(2)}) copy-start(f32[6,6,1536]{2,1,0:T(8,128)} %get-tuple-element.152) | copy-start | bytes 663556
  196.9 58.0 %copy-start.7 = (f32[6,6,1536]{2,1,0:T(8,128)S(1)}, f32[6,6,1536]{2,1,0:T(8,128)}, u32[]{:S(2)}) copy-start(f32[6,6,1536]{2,1,0:T(8,128)} %get-tuple-element.154) | copy-start | bytes 663556
  196.9 58.0 %copy-start.8 = (pred[4,6,6,1536]{3,2,1,0:T(8,128)(4,1)S(1)}, pred[4,6,6,1536]{3,2,1,0:T(8,128)(4,1)}, u32[]{:S(2)}) copy-start(pred[4,6,6,1536]{3,2,1,0:T(8,128)(4,1)} %get-tuple-element.37) | copy-start | bytes 663556
  264.6 31.2 %collective-permute-start.9 = (f32[4,3,6,1536]{3,0,2,1:T(4,128)S(1)}, f32[4,3,6,1536]{3,0,2,1:T(4,128)S(1)}, u32[]{:S(2)}, u32[]{:S(2)}) collective-permute-start(f32[4,3,6,1536]{3,0,2,1:T(4,128)S(1)} %copy.129), channel_id=1, source_target_pairs={{8,0},{16,8},{24,16},{0,24},{9,1},{17,9},{25,17},{1,25},{10,2},{18... | collective-permute-start | bytes 1327112 | tf_op jit(solution)/shard_map/ppermute | solution.py:26
  267.3 28.6 %collective-permute-start.8 = (f32[4,3,6,1536]{3,0,2,1:T(4,128)S(1)}, f32[4,3,6,1536]{3,0,2,1:T(4,128)S(1)}, u32[]{:S(2)}, u32[]{:S(2)}) collective-permute-start(f32[4,3,6,1536]{3,0,2,1:T(4,128)S(1)} %copy.127), channel_id=1, source_target_pairs={{0,8},{8,16},{16,24},{24,0},{1,9},{9,17},{17,25},{25,1},{2,10},{10... | collective-permute-start | bytes 1327112 | tf_op jit(solution)/shard_map/ppermute | solution.py:25
  297.4 18.6 %collective-permute-start.11 = (f32[4,12,3,1536]{3,0,2,1:T(4,128)S(1)}, f32[4,12,3,1536]{3,0,2,1:T(4,128)S(1)}, u32[]{:S(2)}, u32[]{:S(2)}) collective-permute-start(f32[4,12,3,1536]{3,0,2,1:T(4,128)S(1)} %copy.135), channel_id=1, source_target_pairs={{1,0},{2,1},{3,2},{4,3},{5,4},{6,5},{7,6},{0,7},{9,8},{10,9},{11,1... | collective-permute-start | bytes 2654216 | tf_op jit(solution)/shard_map/ppermute | solution.py:26
  298.1 22.0 %collective-permute-start.10 = (f32[4,12,3,1536]{3,0,2,1:T(4,128)S(1)}, f32[4,12,3,1536]{3,0,2,1:T(4,128)S(1)}, u32[]{:S(2)}, u32[]{:S(2)}) collective-permute-start(f32[4,12,3,1536]{3,0,2,1:T(4,128)S(1)} %copy.133), channel_id=1, source_target_pairs={{0,1},{1,2},{2,3},{3,4},{4,5},{5,6},{6,7},{7,0},{8,9},{9,10},{10,1... | collective-permute-start | bytes 2654216 | tf_op jit(solution)/shard_map/ppermute | solution.py:25
  320.5 52.4 %copy-start.46 = (f32[5]{0:T(128)S(1)}, f32[5]{0:T(128)}, u32[]{:S(2)}) copy-start(f32[5]{0:T(128)} %constant.541) | copy-start | bytes 64
  320.5 57.0 %copy-start.4 = (f32[4,6,6,1536]{3,2,1,0:T(8,128)S(1)}, f32[4,6,6,1536]{3,2,1,0:T(8,128)}, u32[]{:S(2)}) copy-start(f32[4,6,6,1536]{3,2,1,0:T(8,128)} %get-tuple-element.7) | copy-start | bytes 2654212
  320.5 57.0 %copy-start.5 = (f32[4,6,6,1536]{3,2,1,0:T(8,128)S(1)}, f32[4,6,6,1536]{3,2,1,0:T(8,128)}, u32[]{:S(2)}) copy-start(f32[4,6,6,1536]{3,2,1,0:T(8,128)} %get-tuple-element.8) | copy-start | bytes 2654212
  320.5 57.0 %copy-start.42 = (f32[4,6]{1,0:T(4,128)S(1)}, f32[4,6]{1,0:T(4,128)}, u32[]{:S(2)}) copy-start(f32[4,6]{1,0:T(4,128)} %get-tuple-element.160) | copy-start | bytes 292
  (35 other events, 264.5 us)
where the time goes:
time: 392 us; the launch traced here: 385 us
  other arithmetic  166 us (42%)
  blocking collectives  118 us (30%)
  local copies, waits for them, and re-layouts  38.5 us (10%)
  waiting for transfers between devices  32.4 us (8%)
  between operations  16.9 us (4%)
  starting transfers between devices  13.2 us (3%)
    reduce_max x15, other arithmetic, finish(): peaks.append(jnp.max(speed))  134 us
    pmax x3, blocking collectives, finish(): bounds = lax.pmax(jnp.stack(peaks), ('gx', 'gy'))  118 us
    ppermute x6, waiting for transfers between devices, with_halo(): after = lax.ppermute(leading, axis, down)  24.5 us
    select_n x3, other arithmetic, finish(): jnp.where(obstacle_part == 1, jnp.maximum(advanced, 0.5), advanced)  18.8 us
    another operation x3, local copies, waits for them, and re-layouts, finish(): bounds = lax.pmax(jnp.stack(peaks), ('gx', 'gy'))  9.83 us
    ppermute x6, starting transfers between devices, with_halo(): after = lax.ppermute(leading, axis, down)  8.44 us
    ppermute x6, waiting for transfers between devices, with_halo(): before = lax.ppermute(last, axis, up)  7.93 us
  transfers between devices with their start and end apart: 12, of which 5 were waited for; matrix products, arithmetic and copies ran while one was open for 30% of the time, Pallas kernels for 0%

commit v1 on v0

v1 whole, which is shorter than its diff:
```python
import functools
import math

import jax
import jax.numpy as jnp
from jax import lax
from jax.experimental import pallas as pl
from jax.experimental.pallas import tpu as pltpu
from jax.sharding import PartitionSpec as P

N3 = 32
N4 = 48
GRID = 96
STEPS = 3
COURANT = 0.5
EPS = 0.75e-6
LANES = 8 * N4


def wave(vs):
    n = len(vs) - 6
    d = [vs[k + 1] - vs[k] for k in range(n + 5)]
    f = [d[k + 1] - d[k] for k in range(n + 4)]
    e = [f[k + 1] - f[k] for k in range(n + 3)]
    j = [e[k + 1] - e[k] for k in range(n + 2)]
    k15 = [1.5 * x for x in f]
    base = [e[k] * e[k] + (0.5 * k15[k] * f[k + 1] + EPS) for k in range(n + 3)]
    left, mid, right = [], [], []
    for k in range(n + 1):
        a = base[k] + k15[k + 1] * e[k]
        b = base[k + 1]
        c = base[k + 2] - k15[k + 2] * e[k + 2]
        left.append(a * a)
        mid.append(b * b)
        right.append(c * c)
    low, high = [], []
    for k in range(n + 1):
        bc = mid[k] * right[k]
        ab = left[k] * mid[k]
        ac = 6.0 * (left[k] * right[k])
        n1 = bc * j[k]
        n2 = ab * j[k + 1]
        total = bc + ab
        both = n1 + n2
        both = both + both
        core = total + ac
        low.append((both + n2) / (core + (ab + ab)) if k < n else None)
        high.append((both + n1) / (core + (bc + bc)) if k > 0 else None)
    out = []
    for i in range(n):
        rm, rp = low[i], high[i + 1]
        center = 6.0 * (vs[i + 4] - vs[i + 2])
        middle = center - (e[i + 1] + e[i + 2]) + (rp - rm)
        jump = (rp + rm) - j[i + 1]
        out.append((middle, jump))
    return out


def tally(middle, jump, drift, kappa):
    gap = drift - middle
    return jnp.abs(gap) + jnp.abs(jump), (kappa * middle) * (drift + gap)


def unsplit_kernel(kappa_ref, v_ref, f0_ref, f3_ref, f4_ref, h_ref, q_ref, peak_ref, up_ref):
    planes, rows, cols, width = v_ref.shape
    lane = lax.broadcasted_iota(jnp.int32, (1, width), 1)
    third, fourth = lane // N4, lane % N4
    peak_ref[...] = jnp.zeros_like(peak_ref)

    def per_row(r, carry):
        def shift(p, carry):
            v = v_ref[p, r]
            for base, stride, place, extent in ((0, N4, third, width // N4), (6, 1, fourth, N4)):
                now = v
                for s in range(1, 4):
                    now = jnp.where(place + s < extent, pltpu.roll(v, width - s * stride, 1), now)
                    up_ref[base + 2 + s, p] = now
                now = v
                for s in range(1, 4):
                    now = jnp.where(place >= s, pltpu.roll(v, s * stride, 1), now)
                    up_ref[base + 3 - s, p] = now
            return carry

        lax.fori_loop(0, planes, shift, 0)

        def per_group(g, carry):
            at = pl.ds(pl.multiple_of(g * LANES, 128), LANES)
            vs = [v_ref[p, r, :, at] for p in range(planes)]
            drift = f0_ref[r, :, at]
            top = peak_ref[0]
            cells = wave([vs[0]] * 3 + vs + [vs[-1]] * 3)
            for p in range(planes):
                speed, part = tally(*cells[p], drift, kappa_ref[0])
                top = jnp.maximum(top, speed)
                h_ref[p, r, :, at] = part
                q_ref[0, p, r, :, at] = cells[p][1]
            peak_ref[0] = top

            def per_plane(p, carry):
                v = v_ref[p, r, :, at]
                total = h_ref[p, r, :, at]
                for slot, base, number in ((1, 0, 3), (2, 6, 4)):
                    around = [up_ref[base + k, p, :, at] for k in range(6)]
                    ((middle, jump),) = wave(around[:3] + [v] + around[3:])
                    drift = f3_ref[p, :, :] if number == 3 else f4_ref[r, :, at]
                    speed, part = tally(middle, jump, drift, kappa_ref[number])
                    peak_ref[slot] = jnp.maximum(peak_ref[slot], speed)
                    q_ref[slot, p, r, :, at] = jump
                    total = total + part
                h_ref[p, r, :, at] = total
                return carry

            lax.fori_loop(0, planes, per_plane, 0)
            return carry

        lax.fori_loop(0, width // LANES, per_group, 0)
        return carry

    lax.fori_loop(0, rows, per_row, 0)


def split_kernel(
    kappa_ref, v_ref, a_lo, a_hi, b_lo, b_hi, f1_ref, f2_ref, hin_ref, h_ref, q_ref, peak_ref, ext_ref
):
    planes, rows, cols, width = v_ref.shape
    peak_ref[...] = jnp.zeros_like(peak_ref)

    def per_plane(p, carry):
        def fill(r, carry):
            ext_ref[r, 0:3, :] = b_lo[p, r]
            ext_ref[r, 3 : 3 + cols, :] = v_ref[p, r]
            ext_ref[r, 3 + cols : 6 + cols, :] = b_hi[p, r]
            return carry

        lax.fori_loop(0, rows, fill, 0)

        def per_group(g, carry):
            at = pl.ds(pl.multiple_of(g * LANES, 128), LANES)
            vs = [a_lo[p, k, :, at] for k in range(3)]
            vs += [v_ref[p, r, :, at] for r in range(rows)]
            vs += [a_hi[p, k, :, at] for k in range(3)]
            top = peak_ref[0]
            drift = f1_ref[p, :, at]
            for r, (middle, jump) in enumerate(wave(vs)):
                speed, part = tally(middle, jump, drift, kappa_ref[1])
                top = jnp.maximum(top, speed)
                h_ref[p, r, :, at] = hin_ref[p, r, :, at] + part
                q_ref[0, p, r, :, at] = jump
            peak_ref[0] = top

            def per_row(r, carry):
                around = [ext_ref[r, k : k + cols, at] for k in range(7)]
                ((middle, jump),) = wave(around)
                speed, part = tally(middle, jump, f2_ref[r, :, at], kappa_ref[2])
                peak_ref[1] = jnp.maximum(peak_ref[1], speed)
                h_ref[p, r, :, at] = h_ref[p, r, :, at] + part
                q_ref[1, p, r, :, at] = jump
                return carry

            lax.fori_loop(0, rows, per_row, 0)
            return carry

        lax.fori_loop(0, width // LANES, per_group, 0)
        return carry

    lax.fori_loop(0, planes, per_plane, 0)


def move_kernel(scale_ref, v_ref, h_ref, qu_ref, qs_ref, target_ref, obstacle_ref, out_ref):
    planes, rows, cols, width = v_ref.shape

    def per_cell(i, carry):
        p, r = i // rows, i % rows
        change = scale_ref[0] * h_ref[p, r]
        change = change - scale_ref[1] * qu_ref[0, p, r] - scale_ref[2] * qs_ref[0, p, r]
        change = change - scale_ref[3] * qs_ref[1, p, r] - scale_ref[4] * qu_ref[1, p, r]
        change = change - scale_ref[5] * qu_ref[2, p, r]
        new = v_ref[p, r] - change
        new = jnp.where(target_ref[p, r] == 1, jnp.minimum(new, -0.5), new)
        out_ref[p, r] = jnp.where(obstacle_ref[p, r] == 1, jnp.maximum(new, 0.5), new)
        return carry

    lax.fori_loop(0, planes * rows, per_cell, 0)


VMEM = pl.BlockSpec(memory_space=pltpu.VMEM)
SMEM = pl.BlockSpec(memory_space=pltpu.SMEM)


def call(kernel, ins, outs, scratch, flops, args):
    return pl.pallas_call(
        kernel,
        out_shape=[jax.ShapeDtypeStruct(s, jnp.float32) for s in outs],
        in_specs=[SMEM] + [VMEM] * ins,
        out_specs=[VMEM] * len(outs),
        scratch_shapes=scratch,
        cost_estimate=pl.CostEstimate(flops=flops, bytes_accessed=1 << 20, transcendentals=0),
        compiler_params=pltpu.CompilerParams(vmem_limit_bytes=40 << 20),
    )(*args)


def drifts(shape, gains):
    planes, rows, cols, width = shape
    one = 2.0 * math.pi / (rows * lax.axis_size("gx"))
    two = 2.0 * math.pi / (cols * lax.axis_size("gy"))
    row = lax.axis_index("gx") * rows + jnp.arange(rows, dtype=jnp.int32)
    col = lax.axis_index("gy") * cols + jnp.arange(cols, dtype=jnp.int32)
    first = (jnp.arange(planes, dtype=jnp.float32) - planes / 2 + 0.5) * (2.0 / GRID)
    a = (one * row.astype(jnp.float32)).reshape(rows, 1, 1)
    b = (two * col.astype(jnp.float32)).reshape(1, cols, 1)
    lane = jnp.arange(width, dtype=jnp.int32)
    third = ((lane // N4).astype(jnp.float32) - N3 / 2 + 0.5) * (2.0 / GRID)
    fourth = ((lane % N4).astype(jnp.float32) - N4 / 2 + 0.5) * (2.0 / GRID)
    third, fourth = third.reshape(1, 1, -1), fourth.reshape(1, 1, -1)
    x0 = first.reshape(planes, 1, 1)
    f3 = gains[3] * (jnp.sin(b) - x0)
    return [
        gains[0] * (jnp.cos(a) - 0.5 * jnp.cos(b) + third),
        gains[1] * (fourth - 0.3 * x0),
        gains[2] * (third + 0.5 * jnp.sin(a)),
        jnp.broadcast_to(f3, (planes, cols, LANES)),
        gains[4] * (jnp.cos(a) * jnp.sin(b) - fourth),
    ]


def exchange(part_lo, part_hi, axis):
    devices = lax.axis_size(axis)
    up = [(i, (i + 1) % devices) for i in range(devices)]
    down = [(k, i) for i, k in up]
    return lax.ppermute(part_hi, axis, up), lax.ppermute(part_lo, axis, down)


def body(value, target, obstacle, gains, costs):
    shape = value.shape
    planes, rows, cols, width = shape
    h = jnp.array(
        [
            2.0 / GRID,
            2.0 * math.pi / (rows * lax.axis_size("gx")),
            2.0 * math.pi / (cols * lax.axis_size("gy")),
            2.0 / GRID,
            2.0 / GRID,
        ],
        dtype=jnp.float32,
    )
    kappa = costs / (288.0 * h)
    f = [d * (12.0 / costs[i]) for i, d in enumerate(drifts(shape, gains))]
    wide = (cols, LANES)
    steps = []
    for _ in range(STEPS):
        a_lo, a_hi = exchange(value[:, :3], value[:, -3:], "gx")
        b_lo, b_hi = exchange(value[:, :, :3], value[:, :, -3:], "gy")
        part, q_un, peak_un = call(
            unsplit_kernel,
            4,
            [shape, (3,) + shape, (3,) + wide],
            [pltpu.VMEM((12, planes, cols, width), jnp.float32)],
            1 << 28,
            (kappa, value, f[0], f[3], f[4]),
        )
        part, q_sp, peak_sp = call(
            split_kernel,
            8,
            [shape, (2,) + shape, (2,) + wide],
            [pltpu.VMEM((rows, cols + 6, width), jnp.float32)],
            1 << 27,
            (kappa, value, a_lo, a_hi, b_lo, b_hi, f[1], f[2], part),
        )
        top_un = jnp.max(peak_un, axis=(1, 2))
        top_sp = jnp.max(peak_sp, axis=(1, 2))
        top = jnp.stack([top_un[0], top_sp[0], top_sp[1], top_un[1], top_un[2]])
        bounds = lax.pmax(top, ("gx", "gy")) * (costs / 12.0)
        dt = COURANT / (jnp.sum(bounds / h) + 1e-6)
        scales = jnp.concatenate([dt[None], dt * bounds / (12.0 * h)])
        (value,) = call(
            move_kernel, 6, [shape], [], 1 << 24,
            (scales, value, part, q_un, q_sp, target, obstacle),
        )
        steps.append(dt)
    return value, jnp.stack(steps)


def solution(mesh):
    spec = P(None, "gx", "gy", None)
    return jax.shard_map(
        body,
        mesh=mesh,
        in_specs=(spec, spec, spec, P(), P()),
        out_specs=(spec, P()),
        check_vma=False,
    )
```

time: 392 us -> 334 us (0.85); the launches traced: 385 us -> 333 us
  other arithmetic: 166 us -> 13.3 us
  Pallas kernels: 0 us -> 111 us
  waiting for transfers between devices: 32.4 us -> 0.03 us
  local copies, waits for them, and re-layouts: 38.5 us -> 66.3 us
  between operations: 16.9 us -> 6.54 us
  starting transfers between devices: 13.2 us -> 20.1 us
    reduce_max x15 -> x6, other arithmetic: 134 us -> 3.38 us  [the longest x3 1.78 us: body(): top_sp = jnp.max(peak_sp, axis=(1, 2))]
    pallas_call x0 -> x9, Pallas kernels: none -> 111 us  [call(): pl.pallas_call(kernel, out_shape=[jax.ShapeDtypeStruct(s, jnp.float32) fo...]
    unnamed x96 -> x112, local copies, waits for them, and re-layouts: 4.45 us -> 38 us
    ppermute x12, waiting for transfers between devices: 32.4 us -> 0.03 us  [exchange(): return (lax.ppermute(part_hi, axis, up), lax.ppermute(part_lo, axis, down))]
    select_n x3 -> x0, other arithmetic: 18.8 us -> none  [finish(): jnp.where(obstacle_part == 1, jnp.maximum(advanced, 0.5), advanced)]
    another operation x3 -> x0, local copies, waits for them, and re-layouts: 9.83 us -> none  [finish(): bounds = lax.pmax(jnp.stack(peaks), ('gx', 'gy'))]
    ppermute x10 -> x12, local copies, waits for them, and re-layouts: 3.32 us -> 12.5 us  [exchange(): return (lax.ppermute(part_hi, axis, up), lax.ppermute(part_lo, axis, down))]
    ppermute x12, starting transfers between devices: 13.2 us -> 20.1 us  [exchange(): return (lax.ppermute(part_hi, axis, up), lax.ppermute(part_lo, axis, down))]
  transfers between devices with their start and end apart: 12 -> 12, of which waited for: 5 -> 0; matrix products, arithmetic and copies ran while one was open for 30% -> 7% of each run, Pallas kernels for 0% -> 16%
where the time goes in v1:
time: 334 us; the launch traced here: 333 us
  blocking collectives  116 us (35%)
  Pallas kernels  111 us (33%)
  local copies, waits for them, and re-layouts  66.3 us (20%)
  starting transfers between devices  20.1 us (6%)
  other arithmetic  13.3 us (4%)
  between operations  6.54 us (2%)
    pmax x3, blocking collectives, body(): bounds = lax.pmax(top, ('gx', 'gy')) * (costs / 12.0)  116 us
    pallas_call x9, Pallas kernels, call(): pl.pallas_call(kernel, out_shape=[jax.ShapeDtypeStruct(s, jnp.float32) fo...  111 us
    unnamed x112, local copies, waits for them, and re-layouts  38 us
    ppermute x12, starting transfers between devices, exchange(): return (lax.ppermute(part_hi, axis, up), lax.ppermute(part_lo, axis, down))  20.1 us
    ppermute x12, local copies, waits for them, and re-layouts, exchange(): return (lax.ppermute(part_hi, axis, up), lax.ppermute(part_lo, axis, down))  12.5 us
  transfers between devices with their start and end apart: 12, of which 0 were waited for; matrix products, arithmetic and copies ran while one was open for 7% of the time, Pallas kernels for 16%

profile of v1, /device:TPU:0, one launch (start us, length us, event | category | flops | bytes accessed | tf_op | source)
XLA Modules:
  0.0 333.0 jit_solution(3620095826315068253)
XLA Ops:
  0.6 2.2 fusion.25
  2.9 3.9 %collective-permute-start.1 = (f32[4,3,6,1536]{3,0,2,1:T(4,128)}, f32[4,3,6,1536]{3,0,2,1:T(4,128)}, u32[]{:S(2)}, u32[]{:S(2)}) collective-permute-start(f32[4,3,6,1536]{3,0,2,1:T(4,128)} %get-tuple-element.52), channel_id=1, source_target_pairs={{8,0},{16,8},{24,16},{0,24},{9,1},{17,9},{25,17},{1,25},{10,2},{18... | collective-permute-start | bytes 1327112 | tf_op jit(solution)/shard_map/ppermute | solution.py:230
  7.8 2.8 collective-permute-start.3
  18.5 17.6 %shard_map.77 = (f32[4,6,6,1536]{3,2,1,0:T(8,128)S(1)}, f32[3,4,6,6,1536]{4,3,2,1,0:T(8,128)S(1)}, f32[3,6,384]{2,1,0:T(8,128)S(1)}) custom-call(f32[5]{0:T(128)S(1)} %multiply.6.kappa_ref, f32[4,6,6,1536]{3,2,1,0:T(8,128)S(1)} %copy.22.v_ref, f32[6,6,1536]{2,1,0:T(8,128)S(1)} %multiply_multiply_fusion.1.f0_ref, f32[4,6,384]{2,1,0:T(8,128)S(1)} %broadcast_in_dim.14.f3_ref, ...), custom_call_target="tpu_custom_call" | custom-call | flops 268435456 | bytes 1048576 | tf_op jit(solution)/shard_map/pallas_call | solution.py:191
  36.9 1.7 copy-done.13
  46.4 17.7 %shard_map.78 = (f32[4,6,6,1536]{3,2,1,0:T(8,128)S(1)}, f32[2,4,6,6,1536]{4,3,2,1,0:T(8,128)S(1)}, f32[2,6,384]{2,1,0:T(8,128)S(1)}) custom-call(f32[5]{0:T(128)S(1)} %multiply.6.kappa_ref, f32[4,6,6,1536]{3,2,1,0:T(8,128)S(1)} %copy.22.v_ref, f32[4,3,6,1536]{3,2,1,0:T(8,128)S(1)} %copy.24.a_lo, f32[4,3,6,1536]{3,2,1,0:T(8,128)S(1)} %copy.25.a_hi, ...), custom_call_target="tpu_custom_call" | custom-call | flops 134217728 | bytes 1048576 | tf_op jit(solution)/shard_map/pallas_call | solution.py:191
  67.0 39.0 %pmax.21 = f32[5]{0:T(128)S(1)} all-reduce(f32[5]{0:T(128)S(1)} %pad_maximum_fusion), channel_id=1, replica_groups=mesh['gx'=4,'gy'=8] {'gx','gy'}, use_global_device_ids=true, to_apply=%region_2.3 | all-reduce | flops 5 | bytes 40 | tf_op jit(solution)/shard_map/pmax | solution.py:272
  108.7 2.0 copy-done.14
  117.8 3.5 %collective-permute-start.7 = (f32[4,6,3,1536]{3,0,2,1:T(4,128)}, f32[4,6,3,1536]{3,0,2,1:T(4,128)}, u32[]{:S(2)}, u32[]{:S(2)}) collective-permute-start(f32[4,6,3,1536]{3,0,2,1:T(4,128)} %copy.34), channel_id=1, source_target_pairs={{1,0},{2,1},{3,2},{4,3},{5,4},{6,5},{7,6},{0,7},{9,8},{10,9},{11,1... | collective-permute-start | bytes 1327112 | tf_op jit(solution)/shard_map/ppermute | solution.py:230
  122.4 2.3 collective-permute-start.4
  126.6 17.6 %shard_map.80 = (f32[4,6,6,1536]{3,2,1,0:T(8,128)S(1)}, f32[3,4,6,6,1536]{4,3,2,1,0:T(8,128)S(1)}, f32[3,6,384]{2,1,0:T(8,128)S(1)}) custom-call(f32[5]{0:T(128)S(1)} %multiply.6.kappa_ref, f32[4,6,6,1536]{3,2,1,0:T(8,128)S(1)} %shard_map.79.v_ref, f32[6,6,1536]{2,1,0:T(8,128)S(1)} %copy-done.6, f32[4,6,384]{2,1,0:T(8,128)S(1)} %copy-done.34, ...), custom_call_target="tpu_custom_call" | custom-call | flops 268435456 | bytes 1048576 | tf_op jit(solution)/shard_map/pallas_call | solution.py:191
  144.2 1.7 copy-done.15
  154.1 17.6 %shard_map.81 = (f32[4,6,6,1536]{3,2,1,0:T(8,128)S(1)}, f32[2,4,6,6,1536]{4,3,2,1,0:T(8,128)S(1)}, f32[2,6,384]{2,1,0:T(8,128)S(1)}) custom-call(f32[5]{0:T(128)S(1)} %multiply.6.kappa_ref, f32[4,6,6,1536]{3,2,1,0:T(8,128)S(1)} %shard_map.79.v_ref, f32[4,3,6,1536]{3,2,1,0:T(8,128)S(1)} %copy.35.a_lo, f32[4,3,6,1536]{3,2,1,0:T(8,128)S(1)} %copy.36.a_hi, ...), custom_call_target="tpu_custom_call" | custom-call | flops 134217728 | bytes 1048576 | tf_op jit(solution)/shard_map/pallas_call | solution.py:191
  177.0 38.5 %pmax.22 = f32[5]{0:T(128)S(1)} all-reduce(f32[5]{0:T(128)S(1)} %pad_maximum_fusion.2), channel_id=1, replica_groups=mesh['gx'=4,'gy'=8] {'gx','gy'}, use_global_device_ids=true, to_apply=%region_6.7 | all-reduce | flops 5 | bytes 40 | tf_op jit(solution)/shard_map/pmax | solution.py:272
  218.2 2.0 copy-done.16
  227.3 3.5 %collective-permute-start.11 = (f32[4,6,3,1536]{3,0,2,1:T(4,128)}, f32[4,6,3,1536]{3,0,2,1:T(4,128)}, u32[]{:S(2)}, u32[]{:S(2)}) collective-permute-start(f32[4,6,3,1536]{3,0,2,1:T(4,128)} %copy.44), channel_id=1, source_target_pairs={{1,0},{2,1},{3,2},{4,3},{5,4},{6,5},{7,6},{0,7},{9,8},{10,9},{11,1... | collective-permute-start | bytes 1327112 | tf_op jit(solution)/shard_map/ppermute | solution.py:230
  231.9 2.3 collective-permute-start.8
  236.1 17.6 %shard_map.83 = (f32[4,6,6,1536]{3,2,1,0:T(8,128)S(1)}, f32[3,4,6,6,1536]{4,3,2,1,0:T(8,128)S(1)}, f32[3,6,384]{2,1,0:T(8,128)S(1)}) custom-call(f32[5]{0:T(128)S(1)} %multiply.6.kappa_ref, f32[4,6,6,1536]{3,2,1,0:T(8,128)S(1)} %shard_map.82.v_ref, f32[6,6,1536]{2,1,0:T(8,128)S(1)} %copy-done.7, f32[4,6,384]{2,1,0:T(8,128)S(1)} %copy-done.35, ...), custom_call_target="tpu_custom_call" | custom-call | flops 268435456 | bytes 1048576 | tf_op jit(solution)/shard_map/pallas_call | solution.py:191
  253.8 1.7 copy-done.11
  261.0 17.6 %shard_map.84 = (f32[4,6,6,1536]{3,2,1,0:T(8,128)S(1)}, f32[2,4,6,6,1536]{4,3,2,1,0:T(8,128)S(1)}, f32[2,6,384]{2,1,0:T(8,128)S(1)}) custom-call(f32[5]{0:T(128)S(1)} %multiply.6.kappa_ref, f32[4,6,6,1536]{3,2,1,0:T(8,128)S(1)} %shard_map.82.v_ref, f32[4,3,6,1536]{3,2,1,0:T(8,128)S(1)} %copy.45.a_lo, f32[4,3,6,1536]{3,2,1,0:T(8,128)S(1)} %copy.46.a_hi, ...), custom_call_target="tpu_custom_call" | custom-call | flops 134217728 | bytes 1048576 | tf_op jit(solution)/shard_map/pallas_call | solution.py:191
  282.6 1.8 pad_maximum_fusion.4
  284.5 38.4 %pmax.23 = f32[5]{0:T(128)S(1)} all-reduce(f32[5]{0:T(128)} %pad_maximum_fusion.4), channel_id=1, replica_groups=mesh['gx'=4,'gy'=8] {'gx','gy'}, use_global_device_ids=true, to_apply=%region_10.11 | all-reduce | flops 5 | bytes 40 | tf_op jit(solution)/shard_map/pmax | solution.py:272
  324.9 2.0 copy-done.12
  329.8 1.7 shard_map.85
  (189 shorter events, 69.4 us)
Async XLA Ops:
  2.9 38.4 %collective-permute-start.1 = (f32[4,3,6,1536]{3,0,2,1:T(4,128)}, f32[4,3,6,1536]{3,0,2,1:T(4,128)}, u32[]{:S(2)}, u32[]{:S(2)}) collective-permute-start(f32[4,3,6,1536]{3,0,2,1:T(4,128)} %get-tuple-element.52), channel_id=1, source_target_pairs={{8,0},{16,8},{24,16},{0,24},{9,1},{17,9},{25,17},{1,25},{10,2},{18... | collective-permute-start | bytes 1327112 | tf_op jit(solution)/shard_map/ppermute | solution.py:230
  6.8 35.7 %collective-permute-start = (f32[4,3,6,1536]{3,0,2,1:T(4,128)}, f32[4,3,6,1536]{3,0,2,1:T(4,128)}, u32[]{:S(2)}, u32[]{:S(2)}) collective-permute-start(f32[4,3,6,1536]{3,0,2,1:T(4,128)} %get-tuple-element.53), channel_id=1, source_target_pairs={{0,8},{8,16},{16,24},{24,0},{1,9},{9,17},{17,25},{25,1},{2,10},{10... | collective-permute-start | bytes 1327112 | tf_op jit(solution)/shard_map/ppermute | solution.py:230
  7.8 35.9 %collective-permute-start.3 = (f32[4,6,3,1536]{3,0,2,1:T(4,128)}, f32[4,6,3,1536]{3,0,2,1:T(4,128)}, u32[]{:S(2)}, u32[]{:S(2)}) collective-permute-start(f32[4,6,3,1536]{3,0,2,1:T(4,128)} %get-tuple-element.50), channel_id=1, source_target_pairs={{1,0},{2,1},{3,2},{4,3},{5,4},{6,5},{7,6},{0,7},{9,8},{10,9},{11,1... | collective-permute-start | bytes 1327112 | tf_op jit(solution)/shard_map/ppermute | solution.py:230
  10.6 34.4 %collective-permute-start.2 = (f32[4,6,3,1536]{3,0,2,1:T(4,128)}, f32[4,6,3,1536]{3,0,2,1:T(4,128)}, u32[]{:S(2)}, u32[]{:S(2)}) collective-permute-start(f32[4,6,3,1536]{3,0,2,1:T(4,128)} %get-tuple-element.51), channel_id=1, source_target_pairs={{0,1},{1,2},{2,3},{3,4},{4,5},{5,6},{6,7},{7,0},{8,9},{9,10},{10,1... | collective-permute-start | bytes 1327112 | tf_op jit(solution)/shard_map/ppermute | solution.py:230
  11.1 35.2 %copy-start.3 = (f32[4,6,6,1536]{3,2,1,0:T(8,128)}, f32[4,6,6,1536]{3,2,1,0:T(8,128)S(1)}, u32[]{:S(2)}) copy-start(f32[4,6,6,1536]{3,2,1,0:T(8,128)S(1)} %copy.22.v_ref) | copy-start | bytes 2654212
  17.6 24.8 %copy-start.5 = (f32[6,6,1536]{2,1,0:T(8,128)}, f32[6,6,1536]{2,1,0:T(8,128)S(1)}, u32[]{:S(2)}) copy-start(f32[6,6,1536]{2,1,0:T(8,128)S(1)} %multiply_multiply_fusion.1.f0_ref) | copy-start | bytes 663556
  18.5 24.0 %copy-start.33 = (f32[4,6,384]{2,1,0:T(8,128)}, f32[4,6,384]{2,1,0:T(8,128)S(1)}, u32[]{:S(2)}) copy-start(f32[4,6,384]{2,1,0:T(8,128)S(1)} %broadcast_in_dim.14.f3_ref) | copy-start | bytes 110596
  46.3 20.4 %copy-start.47 = (s32[4,6,6,1536]{3,0,2,1:T(4,128)S(1)}, s32[4,6,6,1536]{3,0,2,1:T(4,128)}, u32[]{:S(2)}) copy-start(s32[4,6,6,1536]{3,0,2,1:T(4,128)} %param.8) | copy-start | bytes 2654212
  66.5 39.6 %copy-start.51 = (f32[5]{0:T(128)S(1)}, f32[5]{0:T(128)}, u32[]{:S(2)}) copy-start(f32[5]{0:T(128)} %constant.83) | copy-start | bytes 64
  66.5 40.9 %copy-start.50 = (f32[5]{0:T(128)S(1)}, f32[5]{0:T(128)}, u32[]{:S(2)}) copy-start(f32[5]{0:T(128)} %constant.89) | copy-start | bytes 64
  67.0 48.4 %copy-start = (s32[4,6,6,1536]{3,2,1,0:T(8,128)}, s32[4,6,6,1536]{3,2,1,0:T(8,128)S(1)}, u32[]{:S(2)}) copy-start(s32[4,6,6,1536]{3,2,1,0:T(8,128)S(1)} %copy.30.obstacle_ref) | copy-start | bytes 2654212
  117.8 8.8 %copy-start.34 = (f32[4,6,384]{2,1,0:T(8,128)S(1)}, f32[4,6,384]{2,1,0:T(8,128)}, u32[]{:S(2)}) copy-start(f32[4,6,384]{2,1,0:T(8,128)} %copy-done.33) | copy-start | bytes 110596
  117.8 31.4 %collective-permute-start.6 = (f32[4,6,3,1536]{3,0,2,1:T(4,128)}, f32[4,6,3,1536]{3,0,2,1:T(4,128)}, u32[]{:S(2)}, u32[]{:S(2)}) collective-permute-start(f32[4,6,3,1536]{3,0,2,1:T(4,128)} %copy.33), channel_id=1, source_target_pairs={{0,1},{1,2},{2,3},{3,4},{4,5},{5,6},{6,7},{7,0},{8,9},{9,10},{10,1... | collective-permute-start | bytes 1327112 | tf_op jit(solution)/shard_map/ppermute | solution.py:230
  117.8 32.6 %collective-permute-start.7 = (f32[4,6,3,1536]{3,0,2,1:T(4,128)}, f32[4,6,3,1536]{3,0,2,1:T(4,128)}, u32[]{:S(2)}, u32[]{:S(2)}) collective-permute-start(f32[4,6,3,1536]{3,0,2,1:T(4,128)} %copy.34), channel_id=1, source_target_pairs={{1,0},{2,1},{3,2},{4,3},{5,4},{6,5},{7,6},{0,7},{9,8},{10,9},{11,1... | collective-permute-start | bytes 1327112 | tf_op jit(solution)/shard_map/ppermute | solution.py:230
  122.4 29.3 %collective-permute-start.4 = (f32[4,3,6,1536]{3,0,2,1:T(4,128)}, f32[4,3,6,1536]{3,0,2,1:T(4,128)}, u32[]{:S(2)}, u32[]{:S(2)}) collective-permute-start(f32[4,3,6,1536]{3,0,2,1:T(4,128)} %copy.31), channel_id=1, source_target_pairs={{0,8},{8,16},{16,24},{24,0},{1,9},{9,17},{17,25},{25,1},{2,10},{10... | collective-permute-start | bytes 1327112 | tf_op jit(solution)/shard_map/ppermute | solution.py:230
  125.7 27.2 %collective-permute-start.5 = (f32[4,3,6,1536]{3,0,2,1:T(4,128)}, f32[4,3,6,1536]{3,0,2,1:T(4,128)}, u32[]{:S(2)}, u32[]{:S(2)}) collective-permute-start(f32[4,3,6,1536]{3,0,2,1:T(4,128)} %copy.32), channel_id=1, source_target_pairs={{8,0},{16,8},{24,16},{0,24},{9,1},{17,9},{25,17},{1,25},{10,2},{18... | collective-permute-start | bytes 1327112 | tf_op jit(solution)/shard_map/ppermute | solution.py:230
  227.3 8.8 %copy-start.7 = (f32[6,6,1536]{2,1,0:T(8,128)S(1)}, f32[6,6,1536]{2,1,0:T(8,128)}, u32[]{:S(2)}) copy-start(f32[6,6,1536]{2,1,0:T(8,128)} %copy-done.5) | copy-start | bytes 663556
  227.3 8.8 %copy-start.10 = (f32[6,6,1536]{2,1,0:T(8,128)S(1)}, f32[6,6,1536]{2,1,0:T(8,128)}, u32[]{:S(2)}) copy-start(f32[6,6,1536]{2,1,0:T(8,128)} %copy-done.8) | copy-start | bytes 663556
  227.3 8.8 %copy-start.35 = (f32[4,6,384]{2,1,0:T(8,128)S(1)}, f32[4,6,384]{2,1,0:T(8,128)}, u32[]{:S(2)}) copy-start(f32[4,6,384]{2,1,0:T(8,128)} %copy-done.33) | copy-start | bytes 110596
  227.3 29.9 %collective-permute-start.10 = (f32[4,6,3,1536]{3,0,2,1:T(4,128)}, f32[4,6,3,1536]{3,0,2,1:T(4,128)}, u32[]{:S(2)}, u32[]{:S(2)}) collective-permute-start(f32[4,6,3,1536]{3,0,2,1:T(4,128)} %copy.43), channel_id=1, source_target_pairs={{0,1},{1,2},{2,3},{3,4},{4,5},{5,6},{6,7},{7,0},{8,9},{9,10},{10,1... | collective-permute-start | bytes 1327112 | tf_op jit(solution)/shard_map/ppermute | solution.py:230
  227.3 31.1 %collective-permute-start.11 = (f32[4,6,3,1536]{3,0,2,1:T(4,128)}, f32[4,6,3,1536]{3,0,2,1:T(4,128)}, u32[]{:S(2)}, u32[]{:S(2)}) collective-permute-start(f32[4,6,3,1536]{3,0,2,1:T(4,128)} %copy.44), channel_id=1, source_target_pairs={{1,0},{2,1},{3,2},{4,3},{5,4},{6,5},{7,6},{0,7},{9,8},{10,9},{11,1... | collective-permute-start | bytes 1327112 | tf_op jit(solution)/shard_map/ppermute | solution.py:230
  231.9 27.8 %collective-permute-start.8 = (f32[4,3,6,1536]{3,0,2,1:T(4,128)}, f32[4,3,6,1536]{3,0,2,1:T(4,128)S(1)}, u32[]{:S(2)}, u32[]{:S(2)}) collective-permute-start(f32[4,3,6,1536]{3,0,2,1:T(4,128)} %copy.41), channel_id=1, source_target_pairs={{0,8},{8,16},{16,24},{24,0},{1,9},{9,17},{17,25},{25,1},{2,10},{10... | collective-permute-start | bytes 1327112 | tf_op jit(solution)/shard_map/ppermute | solution.py:230
  235.3 24.7 %collective-permute-start.9 = (f32[4,3,6,1536]{3,0,2,1:T(4,128)}, f32[4,3,6,1536]{3,0,2,1:T(4,128)S(1)}, u32[]{:S(2)}, u32[]{:S(2)}) collective-permute-start(f32[4,3,6,1536]{3,0,2,1:T(4,128)} %copy.42), channel_id=1, source_target_pairs={{8,0},{16,8},{24,16},{0,24},{9,1},{17,9},{25,17},{1,25},{10,2},{18... | collective-permute-start | bytes 1327112 | tf_op jit(solution)/shard_map/ppermute | solution.py:230
  261.0 63.9 %copy-start.2 = (s32[4,6,6,1536]{3,2,1,0:T(8,128)S(1)}, s32[4,6,6,1536]{3,2,1,0:T(8,128)}, u32[]{:S(2)}) copy-start(s32[4,6,6,1536]{3,2,1,0:T(8,128)} %copy-done) | copy-start | bytes 2654212
  (42 other events, 103.1 us)

commit v2 on v1

--- a/solution.py
+++ b/solution.py
@@ -83,18 +83,24 @@
 
         lax.fori_loop(0, planes, shift, 0)
 
-        def per_group(g, carry):
-            at = pl.ds(pl.multiple_of(g * LANES, 128), LANES)
+        def along_planes(g, carry):
+            at = pl.ds(pl.multiple_of(g * 128, 128), 128)
             vs = [v_ref[p, r, :, at] for p in range(planes)]
             drift = f0_ref[r, :, at]
-            top = peak_ref[0]
+            top = peak_ref[0, :, at]
             cells = wave([vs[0]] * 3 + vs + [vs[-1]] * 3)
             for p in range(planes):
                 speed, part = tally(*cells[p], drift, kappa_ref[0])
                 top = jnp.maximum(top, speed)
                 h_ref[p, r, :, at] = part
                 q_ref[0, p, r, :, at] = cells[p][1]
-            peak_ref[0] = top
+            peak_ref[0, :, at] = top
+            return carry
+
+        lax.fori_loop(0, width // 128, along_planes, 0)
+
+        def per_group(g, carry):
+            at = pl.ds(pl.multiple_of(g * LANES, 128), LANES)
 
             def per_plane(p, carry):
                 v = v_ref[p, r, :, at]
@@ -104,7 +110,7 @@
                     ((middle, jump),) = wave(around[:3] + [v] + around[3:])
                     drift = f3_ref[p, :, :] if number == 3 else f4_ref[r, :, at]
                     speed, part = tally(middle, jump, drift, kappa_ref[number])
-                    peak_ref[slot] = jnp.maximum(peak_ref[slot], speed)
+                    peak_ref[slot, :, at] = jnp.maximum(peak_ref[slot, :, at], speed)
                     q_ref[slot, p, r, :, at] = jump
                     total = total + part
                 h_ref[p, r, :, at] = total
@@ -120,39 +126,47 @@
 
 
 def split_kernel(
-    kappa_ref, v_ref, a_lo, a_hi, b_lo, b_hi, f1_ref, f2_ref, hin_ref, h_ref, q_ref, peak_ref, ext_ref
+    kappa_ref, v_ref, a_lo, a_hi, b_lo, b_hi, f1_ref, f2_ref, hin_ref, peak_un_ref,
+    h_ref, q_ref, top_ref, ext_ref, near_ref, peak_ref,
 ):
     planes, rows, cols, width = v_ref.shape
     peak_ref[...] = jnp.zeros_like(peak_ref)
 
     def per_plane(p, carry):
         def fill(r, carry):
-            ext_ref[r, 0:3, :] = b_lo[p, r]
-            ext_ref[r, 3 : 3 + cols, :] = v_ref[p, r]
-            ext_ref[r, 3 + cols : 6 + cols, :] = b_hi[p, r]
+            ext_ref[0:3, :] = b_lo[p, r]
+            ext_ref[3 : 3 + cols, :] = v_ref[p, r]
+            ext_ref[3 + cols : 6 + cols, :] = b_hi[p, r]
+            for k in range(7):
+                near_ref[k, r] = ext_ref[k : k + cols, :]
             return carry
 
         lax.fori_loop(0, rows, fill, 0)
 
-        def per_group(g, carry):
-            at = pl.ds(pl.multiple_of(g * LANES, 128), LANES)
+        def along_rows(g, carry):
+            at = pl.ds(pl.multiple_of(g * 128, 128), 128)
             vs = [a_lo[p, k, :, at] for k in range(3)]
             vs += [v_ref[p, r, :, at] for r in range(rows)]
             vs += [a_hi[p, k, :, at] for k in range(3)]
-            top = peak_ref[0]
+            top = peak_ref[0, :, at]
             drift = f1_ref[p, :, at]
             for r, (middle, jump) in enumerate(wave(vs)):
                 speed, part = tally(middle, jump, drift, kappa_ref[1])
                 top = jnp.maximum(top, speed)
                 h_ref[p, r, :, at] = hin_ref[p, r, :, at] + part
                 q_ref[0, p, r, :, at] = jump
-            peak_ref[0] = top
+            peak_ref[0, :, at] = top
+            return carry
+
+        lax.fori_loop(0, width // 128, along_rows, 0)
+
+        def per_group(g, carry):
+            at = pl.ds(pl.multiple_of(g * LANES, 128), LANES)
 
             def per_row(r, carry):
-                around = [ext_ref[r, k : k + cols, at] for k in range(7)]
-                ((middle, jump),) = wave(around)
+                ((middle, jump),) = wave([near_ref[k, r, :, at] for k in range(7)])
                 speed, part = tally(middle, jump, f2_ref[r, :, at], kappa_ref[2])
-                peak_ref[1] = jnp.maximum(peak_ref[1], speed)
+                peak_ref[1, :, at] = jnp.maximum(peak_ref[1, :, at], speed)
                 h_ref[p, r, :, at] = h_ref[p, r, :, at] + part
                 q_ref[1, p, r, :, at] = jump
                 return carry
@@ -164,6 +178,78 @@
         return carry
 
     lax.fori_loop(0, planes, per_plane, 0)
+    tops = [peak_un_ref[0], peak_ref[0], peak_ref[1], peak_un_ref[1], peak_un_ref[2]]
+    row = lax.broadcasted_iota(jnp.int32, top_ref.shape, 0)
+    out = jnp.zeros(top_ref.shape, jnp.float32)
+    for number, part in enumerate(tops):
+        out = jnp.where(row == number, jnp.max(part), out)
+    top_ref[...] = out
+
+
+def peak_kernel(sizes, own_ref, out_ref, slots, send_sem, recv_sem):
+    nx, ny = sizes
+    n = nx * ny
+    me = lax.axis_index("gx") * ny + lax.axis_index("gy")
+
+    def place(k):
+        other = (me + k) % n
+        return (other // ny, other % ny)
+
+    barrier = pltpu.get_barrier_semaphore()
+
+    def greet(k, carry):
+        pl.semaphore_signal(
+            barrier, inc=1, device_id=place(k), device_id_type=pl.DeviceIdType.MESH
+        )
+        return carry
+
+    lax.fori_loop(1, n, greet, 0)
+    pl.semaphore_wait(barrier, n - 1)
+
+    def copy(k):
+        return pltpu.make_async_remote_copy(
+            src_ref=own_ref,
+            dst_ref=slots.at[k],
+            send_sem=send_sem.at[k],
+            recv_sem=recv_sem.at[k],
+            device_id=place(k),
+            device_id_type=pl.DeviceIdType.MESH,
+        )
+
+    def send(k, carry):
+        copy(k).start()
+        return carry
+
+    lax.fori_loop(1, n, send, 0)
+
+    def take(k, top):
+        copy(k).wait_recv()
+        return jnp.maximum(top, slots[k])
+
+    out_ref[...] = lax.fori_loop(1, n, take, own_ref[...])
+
+    def finish(k, carry):
+        copy(k).wait_send()
+        return carry
+
+    lax.fori_loop(1, n, finish, 0)
+
+
+def peak_everywhere(own):
+    sizes = (lax.axis_size("gx"), lax.axis_size("gy"))
+    n = sizes[0] * sizes[1]
+    return pl.pallas_call(
+        functools.partial(peak_kernel, sizes),
+        out_shape=jax.ShapeDtypeStruct(own.shape, jnp.float32),
+        in_specs=[VMEM],
+        out_specs=VMEM,
+        scratch_shapes=[
+            pltpu.VMEM((n,) + own.shape, jnp.float32),
+            pltpu.SemaphoreType.DMA((n,)),
+            pltpu.SemaphoreType.DMA((n,)),
+        ],
+        compiler_params=pltpu.CompilerParams(collective_id=0, has_side_effects=True),
+    )(own)
 
 
 def move_kernel(scale_ref, v_ref, h_ref, qu_ref, qs_ref, target_ref, obstacle_ref, out_ref):
@@ -245,7 +331,6 @@
     )
     kappa = costs / (288.0 * h)
     f = [d * (12.0 / costs[i]) for i, d in enumerate(drifts(shape, gains))]
-    wide = (cols, LANES)
     steps = []
     for _ in range(STEPS):
         a_lo, a_hi = exchange(value[:, :3], value[:, -3:], "gx")
@@ -253,23 +338,24 @@
         part, q_un, peak_un = call(
             unsplit_kernel,
             4,
-            [shape, (3,) + shape, (3,) + wide],
+            [shape, (3,) + shape, (3, cols, width)],
             [pltpu.VMEM((12, planes, cols, width), jnp.float32)],
             1 << 28,
             (kappa, value, f[0], f[3], f[4]),
         )
-        part, q_sp, peak_sp = call(
+        part, q_sp, top = call(
             split_kernel,
-            8,
-            [shape, (2,) + shape, (2,) + wide],
-            [pltpu.VMEM((rows, cols + 6, width), jnp.float32)],
+            9,
+            [shape, (2,) + shape, (8, 128)],
+            [
+                pltpu.VMEM((cols + 6, width), jnp.float32),
+                pltpu.VMEM((7, rows, cols, width), jnp.float32),
+                pltpu.VMEM((2, cols, width), jnp.float32),
+            ],
             1 << 27,
-            (kappa, value, a_lo, a_hi, b_lo, b_hi, f[1], f[2], part),
-        )
-        top_un = jnp.max(peak_un, axis=(1, 2))
-        top_sp = jnp.max(peak_sp, axis=(1, 2))
-        top = jnp.stack([top_un[0], top_sp[0], top_sp[1], top_un[1], top_un[2]])
-        bounds = lax.pmax(top, ("gx", "gy")) * (costs / 12.0)
+            (kappa, value, a_lo, a_hi, b_lo, b_hi, f[1], f[2], part, peak_un),
+        )
+        bounds = peak_everywhere(top)[:5, 0] * (costs / 12.0)
         dt = COURANT / (jnp.sum(bounds / h) + 1e-6)
         scales = jnp.concatenate([dt[None], dt * bounds / (12.0 * h)])
         (value,) = call(

time: 334 us -> 215 us (0.64)
  blocking collectives: 116 us -> 0 us
  local copies, waits for them, and re-layouts: 66.3 us -> 53.9 us
  Pallas kernels: 111 us -> 123 us
  other arithmetic: 13.3 us -> 9.95 us
    pmax x3 -> x0, blocking collectives: 116 us -> none  [body(): bounds = lax.pmax(top, ('gx', 'gy')) * (costs / 12.0)]
    pallas_call x0 -> x3, Pallas kernels: none -> 32.3 us  [peak_everywhere(): pl.pallas_call(functools.partial(peak_kernel, sizes), out_shape=jax.Shape...]
    pallas_call x9, Pallas kernels: 111 us -> 91.2 us  [call(): pl.pallas_call(kernel, out_shape=[jax.ShapeDtypeStruct(s, jnp.float32) fo...]
    ppermute x12, local copies, waits for them, and re-layouts: 12.5 us -> 6.34 us  [exchange(): return (lax.ppermute(part_hi, axis, up), lax.ppermute(part_lo, axis, down))]
    reduce_max x6 -> x0, other arithmetic: 3.38 us -> none  [the longest x3 1.78 us: body(): top_sp = jnp.max(peak_sp, axis=(1, 2))]
    unnamed x112 -> x110, local copies, waits for them, and re-layouts: 38 us -> 37.6 us
  transfers between devices with their start and end apart: 12 -> 12, of which waited for: 0 -> 0; matrix products, arithmetic and copies ran while one was open for 7% -> 9% of each run, Pallas kernels for 16% -> 26%
where the time goes in v2:
time: 215 us; the launch traced here: 214 us
  Pallas kernels  123 us (57%)
  local copies, waits for them, and re-layouts  53.9 us (25%)
  starting transfers between devices  20.1 us (9%)
  other arithmetic  9.95 us (5%)
  between operations  6.76 us (3%)
    pallas_call x9, Pallas kernels, call(): pl.pallas_call(kernel, out_shape=[jax.ShapeDtypeStruct(s, jnp.float32) fo...  91.2 us
    unnamed x110, local copies, waits for them, and re-layouts  37.6 us
    pallas_call x3, Pallas kernels, peak_everywhere(): pl.pallas_call(functools.partial(peak_kernel, sizes), out_shape=jax.Shape...  32.3 us
    ppermute x12, starting transfers between devices, exchange(): return (lax.ppermute(part_hi, axis, up), lax.ppermute(part_lo, axis, down))  20.1 us
    ppermute x12, local copies, waits for them, and re-layouts, exchange(): return (lax.ppermute(part_hi, axis, up), lax.ppermute(part_lo, axis, down))  6.34 us
  transfers between devices with their start and end apart: 12, of which 0 were waited for; matrix products, arithmetic and copies ran while one was open for 9% of the time, Pallas kernels for 26%

profile of v2, /device:TPU:0, one launch (start us, length us, event | category | flops | bytes accessed | tf_op | source)
XLA Modules:
  0.0 214.2 jit_solution(16312122386508826428)
XLA Ops:
  0.6 2.2 %fusion.23 = (f32[4,3,6,1536]{3,0,2,1:T(4,128)}, f32[4,3,6,1536]{3,0,2,1:T(4,128)}) fusion(f32[4,6,6,1536]{3,0,2,1:T(4,128)} %param.6), kind=kLoop, calls=%fused_computation.54 | loop fusion | bytes 1769472 | tf_op jit(solution)/shard_map/slice | solution.py:336
  2.8 3.9 %collective-permute-start.1 = (f32[4,3,6,1536]{3,0,2,1:T(4,128)}, f32[4,3,6,1536]{3,0,2,1:T(4,128)}, u32[]{:S(2)}, u32[]{:S(2)}) collective-permute-start(f32[4,3,6,1536]{3,0,2,1:T(4,128)} %get-tuple-element.54), channel_id=1, source_target_pairs={{8,0},{16,8},{24,16},{0,24},{9,1},{17,9},{25,17},{1,25},{10,2},{18... | collective-permute-start | bytes 1327112 | tf_op jit(solution)/shard_map/ppermute | solution.py:316
  7.8 2.8 %collective-permute-start.3 = (f32[4,6,3,1536]{3,0,2,1:T(4,128)}, f32[4,6,3,1536]{3,0,2,1:T(4,128)}, u32[]{:S(2)}, u32[]{:S(2)}) collective-permute-start(f32[4,6,3,1536]{3,0,2,1:T(4,128)} %get-tuple-element.52), channel_id=1, source_target_pairs={{1,0},{2,1},{3,2},{4,3},{5,4},{6,5},{7,6},{0,7},{9,8},{10,9},{11,1... | collective-permute-start | bytes 1327112 | tf_op jit(solution)/shard_map/ppermute | solution.py:316
  24.7 18.3 %shard_map.77 = (f32[4,6,6,1536]{3,2,1,0:T(8,128)S(1)}, f32[3,4,6,6,1536]{4,3,2,1,0:T(8,128)S(1)}, f32[3,6,1536]{2,1,0:T(8,128)S(1)}) custom-call(f32[5]{0:T(128)S(1)} %multiply.6.kappa_ref, f32[4,6,6,1536]{3,2,1,0:T(8,128)S(1)} %copy.37.v_ref, f32[6,6,1536]{2,1,0:T(8,128)S(1)} %multiply_multiply_fusion.1.f0_ref, f32[4,6,384]{2,1,0:T(8,128)S(1)} %broadcast_in_dim.14.f3_ref, ...), custom_call_target="tpu_custom_call" | custom-call | flops 268435456 | bytes 1048576 | tf_op jit(solution)/shard_map/pallas_call | solution.py:277
  43.0 1.7 copy-done.13
  50.5 10.4 %shard_map.78 = (f32[4,6,6,1536]{3,2,1,0:T(8,128)S(1)}, f32[2,4,6,6,1536]{4,3,2,1,0:T(8,128)S(1)}, f32[8,128]{1,0:T(8,128)S(1)}) custom-call(f32[5]{0:T(128)S(1)} %multiply.6.kappa_ref, f32[4,6,6,1536]{3,2,1,0:T(8,128)S(1)} %copy.37.v_ref, f32[4,3,6,1536]{3,2,1,0:T(8,128)S(1)} %copy.38.a_lo, f32[4,3,6,1536]{3,2,1,0:T(8,128)S(1)} %copy.39.a_hi, ...), custom_call_target="tpu_custom_call" | custom-call | flops 134217728 | bytes 1048576 | tf_op jit(solution)/shard_map/pallas_call | solution.py:277
  63.9 11.9 %shard_map.79 = f32[8,128]{1,0:T(8,128)} custom-call(f32[8,128]{1,0:T(8,128)} %copy-done.39), custom_call_target="tpu_custom_call" | custom-call | tf_op jit(solution)/shard_map/pallas_call | solution.py:241
  80.0 2.0 copy-done.14
  84.9 1.7 shard_map.80.v_ref
  87.7 3.4 %collective-permute-start.7 = (f32[4,6,3,1536]{3,0,2,1:T(4,128)S(1)}, f32[4,6,3,1536]{3,0,2,1:T(4,128)S(1)}, u32[]{:S(2)}, u32[]{:S(2)}) collective-permute-start(f32[4,6,3,1536]{3,0,2,1:T(4,128)S(1)} %copy.48), channel_id=1, source_target_pairs={{1,0},{2,1},{3,2},{4,3},{5,4},{6,5},{7,6},{0,7},{9,8},{10,9},{11,1... | collective-permute-start | bytes 1327112 | tf_op jit(solution)/shard_map/ppermute | solution.py:316
  94.8 18.3 %shard_map.81 = (f32[4,6,6,1536]{3,2,1,0:T(8,128)S(1)}, f32[3,4,6,6,1536]{4,3,2,1,0:T(8,128)S(1)}, f32[3,6,1536]{2,1,0:T(8,128)S(1)}) custom-call(f32[5]{0:T(128)S(1)} %multiply.6.kappa_ref, f32[4,6,6,1536]{3,2,1,0:T(8,128)S(1)} %shard_map.80.v_ref, f32[6,6,1536]{2,1,0:T(8,128)S(1)} %copy-done.6, f32[4,6,384]{2,1,0:T(8,128)S(1)} %copy-done.30, ...), custom_call_target="tpu_custom_call" | custom-call | flops 268435456 | bytes 1048576 | tf_op jit(solution)/shard_map/pallas_call | solution.py:277
  113.1 1.7 copy-done.15
  116.1 10.4 %shard_map.82 = (f32[4,6,6,1536]{3,2,1,0:T(8,128)S(1)}, f32[2,4,6,6,1536]{4,3,2,1,0:T(8,128)S(1)}, f32[8,128]{1,0:T(8,128)S(1)}) custom-call(f32[5]{0:T(128)S(1)} %multiply.6.kappa_ref, f32[4,6,6,1536]{3,2,1,0:T(8,128)S(1)} %shard_map.80.v_ref, f32[4,3,6,1536]{3,2,1,0:T(8,128)S(1)} %copy.49.a_lo, f32[4,3,6,1536]{3,2,1,0:T(8,128)S(1)} %copy.50.a_hi, ...), custom_call_target="tpu_custom_call" | custom-call | flops 134217728 | bytes 1048576 | tf_op jit(solution)/shard_map/pallas_call | solution.py:277
  129.6 9.9 %shard_map.83 = f32[8,128]{1,0:T(8,128)} custom-call(f32[8,128]{1,0:T(8,128)} %copy-done.40), custom_call_target="tpu_custom_call" | custom-call | tf_op jit(solution)/shard_map/pallas_call | solution.py:241
  143.0 2.0 copy-done.16
  148.0 1.7 shard_map.84.v_ref
  150.7 3.4 %collective-permute-start.11 = (f32[4,6,3,1536]{3,0,2,1:T(4,128)S(1)}, f32[4,6,3,1536]{3,0,2,1:T(4,128)S(1)}, u32[]{:S(2)}, u32[]{:S(2)}) collective-permute-start(f32[4,6,3,1536]{3,0,2,1:T(4,128)S(1)} %copy.58), channel_id=1, source_target_pairs={{1,0},{2,1},{3,2},{4,3},{5,4},{6,5},{7,6},{0,7},{9,8},{10,9},{11,1... | collective-permute-start | bytes 1327112 | tf_op jit(solution)/shard_map/ppermute | solution.py:316
  155.9 2.1 collective-permute-start.9
  158.0 18.3 %shard_map.85 = (f32[4,6,6,1536]{3,2,1,0:T(8,128)S(1)}, f32[3,4,6,6,1536]{4,3,2,1,0:T(8,128)S(1)}, f32[3,6,1536]{2,1,0:T(8,128)S(1)}) custom-call(f32[5]{0:T(128)S(1)} %multiply.6.kappa_ref, f32[4,6,6,1536]{3,2,1,0:T(8,128)S(1)} %shard_map.84.v_ref, f32[6,6,1536]{2,1,0:T(8,128)S(1)} %copy-done.7, f32[4,6,384]{2,1,0:T(8,128)S(1)} %copy-done.31, ...), custom_call_target="tpu_custom_call" | custom-call | flops 268435456 | bytes 1048576 | tf_op jit(solution)/shard_map/pallas_call | solution.py:277
  176.3 1.7 copy-done.11
  179.3 10.4 %shard_map.86 = (f32[4,6,6,1536]{3,2,1,0:T(8,128)S(1)}, f32[2,4,6,6,1536]{4,3,2,1,0:T(8,128)S(1)}, f32[8,128]{1,0:T(8,128)S(1)}) custom-call(f32[5]{0:T(128)S(1)} %multiply.6.kappa_ref, f32[4,6,6,1536]{3,2,1,0:T(8,128)S(1)} %shard_map.84.v_ref, f32[4,3,6,1536]{3,2,1,0:T(8,128)S(1)} %copy.59.a_lo, f32[4,3,6,1536]{3,2,1,0:T(8,128)S(1)} %copy.60.a_hi, ...), custom_call_target="tpu_custom_call" | custom-call | flops 134217728 | bytes 1048576 | tf_op jit(solution)/shard_map/pallas_call | solution.py:277
  192.8 10.5 %shard_map.87 = f32[8,128]{1,0:T(8,128)} custom-call(f32[8,128]{1,0:T(8,128)} %copy-done.38), custom_call_target="tpu_custom_call" | custom-call | tf_op jit(solution)/shard_map/pallas_call | solution.py:241
  206.1 2.0 copy-done.12
  211.0 1.7 shard_map.88
  (178 shorter events, 55.0 us)
Async XLA Ops:
  2.8 42.7 %collective-permute-start.1 = (f32[4,3,6,1536]{3,0,2,1:T(4,128)}, f32[4,3,6,1536]{3,0,2,1:T(4,128)}, u32[]{:S(2)}, u32[]{:S(2)}) collective-permute-start(f32[4,3,6,1536]{3,0,2,1:T(4,128)} %get-tuple-element.54), channel_id=1, source_target_pairs={{8,0},{16,8},{24,16},{0,24},{9,1},{17,9},{25,17},{1,25},{10,2},{18... | collective-permute-start | bytes 1327112 | tf_op jit(solution)/shard_map/ppermute | solution.py:316
  6.8 40.0 %collective-permute-start = (f32[4,3,6,1536]{3,0,2,1:T(4,128)}, f32[4,3,6,1536]{3,0,2,1:T(4,128)}, u32[]{:S(2)}, u32[]{:S(2)}) collective-permute-start(f32[4,3,6,1536]{3,0,2,1:T(4,128)} %get-tuple-element.55), channel_id=1, source_target_pairs={{0,8},{8,16},{16,24},{24,0},{1,9},{9,17},{17,25},{25,1},{2,10},{10... | collective-permute-start | bytes 1327112 | tf_op jit(solution)/shard_map/ppermute | solution.py:316
  7.8 40.1 %collective-permute-start.3 = (f32[4,6,3,1536]{3,0,2,1:T(4,128)}, f32[4,6,3,1536]{3,0,2,1:T(4,128)}, u32[]{:S(2)}, u32[]{:S(2)}) collective-permute-start(f32[4,6,3,1536]{3,0,2,1:T(4,128)} %get-tuple-element.52), channel_id=1, source_target_pairs={{1,0},{2,1},{3,2},{4,3},{5,4},{6,5},{7,6},{0,7},{9,8},{10,9},{11,1... | collective-permute-start | bytes 1327112 | tf_op jit(solution)/shard_map/ppermute | solution.py:316
  10.5 38.6 %collective-permute-start.2 = (f32[4,6,3,1536]{3,0,2,1:T(4,128)}, f32[4,6,3,1536]{3,0,2,1:T(4,128)}, u32[]{:S(2)}, u32[]{:S(2)}) collective-permute-start(f32[4,6,3,1536]{3,0,2,1:T(4,128)} %get-tuple-element.53), channel_id=1, source_target_pairs={{0,1},{1,2},{2,3},{3,4},{4,5},{5,6},{6,7},{7,0},{8,9},{9,10},{10,1... | collective-permute-start | bytes 1327112 | tf_op jit(solution)/shard_map/ppermute | solution.py:316
  13.7 36.7 %copy-start.3 = (f32[4,6,6,1536]{3,2,1,0:T(8,128)}, f32[4,6,6,1536]{3,2,1,0:T(8,128)S(1)}, u32[]{:S(2)}) copy-start(f32[4,6,6,1536]{3,2,1,0:T(8,128)S(1)} %copy.37.v_ref) | copy-start | bytes 2654212
  21.6 57.1 %copy-start = (s32[4,6,6,1536]{3,2,1,0:T(8,128)}, s32[4,6,6,1536]{3,2,1,0:T(8,128)S(1)}, u32[]{:S(2)}) copy-start(s32[4,6,6,1536]{3,2,1,0:T(8,128)S(1)} %copy.44.obstacle_ref) | copy-start | bytes 2654212
  23.1 27.3 %copy-start.32 = (f32[6,1,1536]{2,1,0:T(1,128)}, f32[6,1,1536]{2,1,0:T(1,128)S(1)}, u32[]{:S(2)}) copy-start(f32[6,1,1536]{2,1,0:T(1,128)S(1)} %multiply_multiply_fusion.2.f2_ref) | copy-start | bytes 110596
  23.1 21.6 %copy-start.48 = (f32[4]{0:T(128)S(1)}, f32[4]{0:T(128)}, u32[]{:S(2)}) copy-start(f32[4]{0:T(128)} %fusion.12) | copy-start | bytes 52
  23.9 22.8 %copy-start.5 = (f32[6,6,1536]{2,1,0:T(8,128)}, f32[6,6,1536]{2,1,0:T(8,128)S(1)}, u32[]{:S(2)}) copy-start(f32[6,6,1536]{2,1,0:T(8,128)S(1)} %multiply_multiply_fusion.1.f0_ref) | copy-start | bytes 663556
  24.6 22.1 %copy-start.8 = (f32[6,6,1536]{2,1,0:T(8,128)}, f32[6,6,1536]{2,1,0:T(8,128)S(1)}, u32[]{:S(2)}) copy-start(f32[6,6,1536]{2,1,0:T(8,128)S(1)} %multiply_multiply_fusion.f4_ref) | copy-start | bytes 663556
  24.7 22.0 %copy-start.29 = (f32[4,6,384]{2,1,0:T(8,128)}, f32[4,6,384]{2,1,0:T(8,128)S(1)}, u32[]{:S(2)}) copy-start(f32[4,6,384]{2,1,0:T(8,128)S(1)} %broadcast_in_dim.14.f3_ref) | copy-start | bytes 110596
  50.4 28.1 %copy-start.45 = (f32[5]{0:T(128)S(1)}, f32[5]{0:T(128)}, u32[]{:S(2)}) copy-start(f32[5]{0:T(128)} %constant.87) | copy-start | bytes 64
  87.5 27.3 %collective-permute-start.6 = (f32[4,6,3,1536]{3,0,2,1:T(4,128)S(1)}, f32[4,6,3,1536]{3,0,2,1:T(4,128)S(1)}, u32[]{:S(2)}, u32[]{:S(2)}) collective-permute-start(f32[4,6,3,1536]{3,0,2,1:T(4,128)S(1)} %copy.47), channel_id=1, source_target_pairs={{0,1},{1,2},{2,3},{3,4},{4,5},{5,6},{6,7},{7,0},{8,9},{9,10},{10,1... | collective-permute-start | bytes 1327112 | tf_op jit(solution)/shard_map/ppermute | solution.py:316
  87.7 27.3 %collective-permute-start.7 = (f32[4,6,3,1536]{3,0,2,1:T(4,128)S(1)}, f32[4,6,3,1536]{3,0,2,1:T(4,128)S(1)}, u32[]{:S(2)}, u32[]{:S(2)}) collective-permute-start(f32[4,6,3,1536]{3,0,2,1:T(4,128)S(1)} %copy.48), channel_id=1, source_target_pairs={{1,0},{2,1},{3,2},{4,3},{5,4},{6,5},{7,6},{0,7},{9,8},{10,9},{11,1... | collective-permute-start | bytes 1327112 | tf_op jit(solution)/shard_map/ppermute | solution.py:316
  91.4 23.9 %collective-permute-start.4 = (f32[4,3,6,1536]{3,0,2,1:T(4,128)S(1)}, f32[4,3,6,1536]{3,0,2,1:T(4,128)S(1)}, u32[]{:S(2)}, u32[]{:S(2)}) collective-permute-start(f32[4,3,6,1536]{3,0,2,1:T(4,128)S(1)} %copy.45), channel_id=1, source_target_pairs={{0,8},{8,16},{16,24},{24,0},{1,9},{9,17},{17,25},{25,1},{2,10},{10... | collective-permute-start | bytes 1327112 | tf_op jit(solution)/shard_map/ppermute | solution.py:316
  93.1 22.4 %collective-permute-start.5 = (f32[4,3,6,1536]{3,0,2,1:T(4,128)S(1)}, f32[4,3,6,1536]{3,0,2,1:T(4,128)S(1)}, u32[]{:S(2)}, u32[]{:S(2)}) collective-permute-start(f32[4,3,6,1536]{3,0,2,1:T(4,128)S(1)} %copy.46), channel_id=1, source_target_pairs={{8,0},{16,8},{24,16},{0,24},{9,1},{17,9},{25,17},{1,25},{10,2},{18... | collective-permute-start | bytes 1327112 | tf_op jit(solution)/shard_map/ppermute | solution.py:316
  116.1 24.3 %copy-start.46 = (f32[5]{0:T(128)S(1)}, f32[5]{0:T(128)}, u32[]{:S(2)}) copy-start(f32[5]{0:T(128)} %constant.81) | copy-start | bytes 64
  150.6 7.4 %copy-start.7 = (f32[6,6,1536]{2,1,0:T(8,128)S(1)}, f32[6,6,1536]{2,1,0:T(8,128)}, u32[]{:S(2)}) copy-start(f32[6,6,1536]{2,1,0:T(8,128)} %copy-done.5) | copy-start | bytes 663556
  150.6 27.4 %collective-permute-start.10 = (f32[4,6,3,1536]{3,0,2,1:T(4,128)S(1)}, f32[4,6,3,1536]{3,0,2,1:T(4,128)S(1)}, u32[]{:S(2)}, u32[]{:S(2)}) collective-permute-start(f32[4,6,3,1536]{3,0,2,1:T(4,128)S(1)} %copy.57), channel_id=1, source_target_pairs={{0,1},{1,2},{2,3},{3,4},{4,5},{5,6},{6,7},{7,0},{8,9},{9,10},{10,1... | collective-permute-start | bytes 1327112 | tf_op jit(solution)/shard_map/ppermute | solution.py:316
  150.7 27.5 %collective-permute-start.11 = (f32[4,6,3,1536]{3,0,2,1:T(4,128)S(1)}, f32[4,6,3,1536]{3,0,2,1:T(4,128)S(1)}, u32[]{:S(2)}, u32[]{:S(2)}) collective-permute-start(f32[4,6,3,1536]{3,0,2,1:T(4,128)S(1)} %copy.58), channel_id=1, source_target_pairs={{1,0},{2,1},{3,2},{4,3},{5,4},{6,5},{7,6},{0,7},{9,8},{10,9},{11,1... | collective-permute-start | bytes 1327112 | tf_op jit(solution)/shard_map/ppermute | solution.py:316
  154.5 24.1 %collective-permute-start.8 = (f32[4,3,6,1536]{3,0,2,1:T(4,128)S(1)}, f32[4,3,6,1536]{3,0,2,1:T(4,128)S(1)}, u32[]{:S(2)}, u32[]{:S(2)}) collective-permute-start(f32[4,3,6,1536]{3,0,2,1:T(4,128)S(1)} %copy.55), channel_id=1, source_target_pairs={{0,8},{8,16},{16,24},{24,0},{1,9},{9,17},{17,25},{25,1},{2,10},{10... | collective-permute-start | bytes 1327112 | tf_op jit(solution)/shard_map/ppermute | solution.py:316
  155.9 22.8 %collective-permute-start.9 = (f32[4,3,6,1536]{3,0,2,1:T(4,128)S(1)}, f32[4,3,6,1536]{3,0,2,1:T(4,128)S(1)}, u32[]{:S(2)}, u32[]{:S(2)}) collective-permute-start(f32[4,3,6,1536]{3,0,2,1:T(4,128)S(1)} %copy.56), channel_id=1, source_target_pairs={{8,0},{16,8},{24,16},{0,24},{9,1},{17,9},{25,17},{1,25},{10,2},{18... | collective-permute-start | bytes 1327112 | tf_op jit(solution)/shard_map/ppermute | solution.py:316
  179.3 24.8 %copy-start.47 = (f32[5]{0:T(128)S(1)}, f32[5]{0:T(128)}, u32[]{:S(2)}) copy-start(f32[5]{0:T(128)} %constant.81) | copy-start | bytes 64
  179.3 26.8 %copy-start.2 = (s32[4,6,6,1536]{3,2,1,0:T(8,128)S(1)}, s32[4,6,6,1536]{3,2,1,0:T(8,128)}, u32[]{:S(2)}) copy-start(s32[4,6,6,1536]{3,2,1,0:T(8,128)} %copy-done) | copy-start | bytes 2654212
  (41 other events, 109.8 us)

commit v3 on v2

--- a/solution.py
+++ b/solution.py
@@ -186,14 +186,11 @@
     top_ref[...] = out
 
 
-def peak_kernel(sizes, own_ref, out_ref, slots, send_sem, recv_sem):
-    nx, ny = sizes
-    n = nx * ny
-    me = lax.axis_index("gx") * ny + lax.axis_index("gy")
+def peak_kernel(axis, n, own_ref, out_ref, slots, send_sem, recv_sem):
+    x, y = lax.axis_index("gx"), lax.axis_index("gy")
 
     def place(k):
-        other = (me + k) % n
-        return (other // ny, other % ny)
+        return ((x + k) % n, y) if axis == "gx" else (x, (y + k) % n)
 
     barrier = pltpu.get_barrier_semaphore()
 
@@ -235,11 +232,10 @@
     lax.fori_loop(1, n, finish, 0)
 
 
-def peak_everywhere(own):
-    sizes = (lax.axis_size("gx"), lax.axis_size("gy"))
-    n = sizes[0] * sizes[1]
+def peak_along(own, axis, number):
+    n = lax.axis_size(axis)
     return pl.pallas_call(
-        functools.partial(peak_kernel, sizes),
+        functools.partial(peak_kernel, axis, n),
         out_shape=jax.ShapeDtypeStruct(own.shape, jnp.float32),
         in_specs=[VMEM],
         out_specs=VMEM,
@@ -248,7 +244,7 @@
             pltpu.SemaphoreType.DMA((n,)),
             pltpu.SemaphoreType.DMA((n,)),
         ],
-        compiler_params=pltpu.CompilerParams(collective_id=0, has_side_effects=True),
+        compiler_params=pltpu.CompilerParams(collective_id=number, has_side_effects=True),
     )(own)
 
 
@@ -355,7 +351,8 @@
             1 << 27,
             (kappa, value, a_lo, a_hi, b_lo, b_hi, f[1], f[2], part, peak_un),
         )
-        bounds = peak_everywhere(top)[:5, 0] * (costs / 12.0)
+        top = peak_along(peak_along(top, "gy", 0), "gx", 1)
+        bounds = top[:5, 0] * (costs / 12.0)
         dt = COURANT / (jnp.sum(bounds / h) + 1e-6)
         scales = jnp.concatenate([dt[None], dt * bounds / (12.0 * h)])
         (value,) = call(

time: 215 us -> 222 us (1.033)
  Pallas kernels: 123 us -> 130 us
    pallas_call x3 -> x6, Pallas kernels: 32.3 us -> 39 us  [peak_along(): pl.pallas_call(functools.partial(peak_kernel, axis, n), out_shape=jax.Sha...]
  transfers between devices with their start and end apart: 12 -> 12, of which waited for: 0 -> 0; matrix products, arithmetic and copies ran while one was open for 9% -> 8% of each run, Pallas kernels for 26% -> 25%
where the time goes in v3:
time: 222 us; the launch traced here: 221 us
  Pallas kernels  130 us (59%)
  local copies, waits for them, and re-layouts  53.9 us (24%)
  starting transfers between devices  20.1 us (9%)
  other arithmetic  9.95 us (4%)
  between operations  6.8 us (3%)
    pallas_call x9, Pallas kernels, call(): pl.pallas_call(kernel, out_shape=[jax.ShapeDtypeStruct(s, jnp.float32) fo...  91.2 us
    pallas_call x6, Pallas kernels, peak_along(): pl.pallas_call(functools.partial(peak_kernel, axis, n), out_shape=jax.Sha...  39 us
    unnamed x110, local copies, waits for them, and re-layouts  37.6 us
    ppermute x12, starting transfers between devices, exchange(): return (lax.ppermute(part_hi, axis, up), lax.ppermute(part_lo, axis, down))  20.1 us
    ppermute x12, local copies, waits for them, and re-layouts, exchange(): return (lax.ppermute(part_hi, axis, up), lax.ppermute(part_lo, axis, down))  6.34 us
  transfers between devices with their start and end apart: 12, of which 0 were waited for; matrix products, arithmetic and copies ran while one was open for 8% of the time, Pallas kernels for 25%

profile of v3, /device:TPU:0, one launch (start us, length us, event | category | flops | bytes accessed | tf_op | source)
XLA Modules:
  0.0 220.9 jit_solution(1676572354251812021)
XLA Ops:
  0.6 2.2 fusion.23
  2.8 3.9 %collective-permute-start.1 = (f32[4,3,6,1536]{3,0,2,1:T(4,128)}, f32[4,3,6,1536]{3,0,2,1:T(4,128)}, u32[]{:S(2)}, u32[]{:S(2)}) collective-permute-start(f32[4,3,6,1536]{3,0,2,1:T(4,128)} %get-tuple-element.54), channel_id=1, source_target_pairs={{8,0},{16,8},{24,16},{0,24},{9,1},{17,9},{25,17},{1,25},{10,2},{18... | collective-permute-start | bytes 1327112 | tf_op jit(solution)/shard_map/ppermute | solution.py:312
  7.8 2.8 %collective-permute-start.3 = (f32[4,6,3,1536]{3,0,2,1:T(4,128)}, f32[4,6,3,1536]{3,0,2,1:T(4,128)}, u32[]{:S(2)}, u32[]{:S(2)}) collective-permute-start(f32[4,6,3,1536]{3,0,2,1:T(4,128)} %get-tuple-element.52), channel_id=1, source_target_pairs={{1,0},{2,1},{3,2},{4,3},{5,4},{6,5},{7,6},{0,7},{9,8},{10,9},{11,1... | collective-permute-start | bytes 1327112 | tf_op jit(solution)/shard_map/ppermute | solution.py:312
  24.7 18.3 %shard_map.77 = (f32[4,6,6,1536]{3,2,1,0:T(8,128)S(1)}, f32[3,4,6,6,1536]{4,3,2,1,0:T(8,128)S(1)}, f32[3,6,1536]{2,1,0:T(8,128)S(1)}) custom-call(f32[5]{0:T(128)S(1)} %multiply.6.kappa_ref, f32[4,6,6,1536]{3,2,1,0:T(8,128)S(1)} %copy.37.v_ref, f32[6,6,1536]{2,1,0:T(8,128)S(1)} %multiply_multiply_fusion.1.f0_ref, f32[4,6,384]{2,1,0:T(8,128)S(1)} %broadcast_in_dim.14.f3_ref, ...), custom_call_target="tpu_custom_call" | custom-call | flops 268435456 | bytes 1048576 | tf_op jit(solution)/shard_map/pallas_call | solution.py:273
  43.0 1.7 copy-done.13
  50.5 10.4 %shard_map.78 = (f32[4,6,6,1536]{3,2,1,0:T(8,128)S(1)}, f32[2,4,6,6,1536]{4,3,2,1,0:T(8,128)S(1)}, f32[8,128]{1,0:T(8,128)S(1)}) custom-call(f32[5]{0:T(128)S(1)} %multiply.6.kappa_ref, f32[4,6,6,1536]{3,2,1,0:T(8,128)S(1)} %copy.37.v_ref, f32[4,3,6,1536]{3,2,1,0:T(8,128)S(1)} %copy.38.a_lo, f32[4,3,6,1536]{3,2,1,0:T(8,128)S(1)} %copy.39.a_hi, ...), custom_call_target="tpu_custom_call" | custom-call | flops 134217728 | bytes 1048576 | tf_op jit(solution)/shard_map/pallas_call | solution.py:273
  63.9 7.2 %shard_map.79.own_ref = f32[8,128]{1,0:T(8,128)} custom-call(f32[8,128]{1,0:T(8,128)} %copy-done.39), custom_call_target="tpu_custom_call" | custom-call | tf_op jit(solution)/shard_map/pallas_call | solution.py:237
  71.2 6.2 %shard_map.80 = f32[8,128]{1,0:T(8,128)} custom-call(f32[8,128]{1,0:T(8,128)} %shard_map.79.own_ref), custom_call_target="tpu_custom_call" | custom-call | tf_op jit(solution)/shard_map/pallas_call | solution.py:237
  81.5 2.0 copy-done.14
  89.1 3.5 %collective-permute-start.7 = (f32[4,6,3,1536]{3,0,2,1:T(4,128)S(1)}, f32[4,6,3,1536]{3,0,2,1:T(4,128)S(1)}, u32[]{:S(2)}, u32[]{:S(2)}) collective-permute-start(f32[4,6,3,1536]{3,0,2,1:T(4,128)S(1)} %copy.48), channel_id=1, source_target_pairs={{1,0},{2,1},{3,2},{4,3},{5,4},{6,5},{7,6},{0,7},{9,8},{10,9},{11,1... | collective-permute-start | bytes 1327112 | tf_op jit(solution)/shard_map/ppermute | solution.py:312
  96.3 18.3 %shard_map.82 = (f32[4,6,6,1536]{3,2,1,0:T(8,128)S(1)}, f32[3,4,6,6,1536]{4,3,2,1,0:T(8,128)S(1)}, f32[3,6,1536]{2,1,0:T(8,128)S(1)}) custom-call(f32[5]{0:T(128)S(1)} %multiply.6.kappa_ref, f32[4,6,6,1536]{3,2,1,0:T(8,128)S(1)} %shard_map.81.v_ref, f32[6,6,1536]{2,1,0:T(8,128)S(1)} %copy-done.6, f32[4,6,384]{2,1,0:T(8,128)S(1)} %copy-done.30, ...), custom_call_target="tpu_custom_call" | custom-call | flops 268435456 | bytes 1048576 | tf_op jit(solution)/shard_map/pallas_call | solution.py:273
  114.6 1.7 copy-done.15
  117.6 10.4 %shard_map.83 = (f32[4,6,6,1536]{3,2,1,0:T(8,128)S(1)}, f32[2,4,6,6,1536]{4,3,2,1,0:T(8,128)S(1)}, f32[8,128]{1,0:T(8,128)S(1)}) custom-call(f32[5]{0:T(128)S(1)} %multiply.6.kappa_ref, f32[4,6,6,1536]{3,2,1,0:T(8,128)S(1)} %shard_map.81.v_ref, f32[4,3,6,1536]{3,2,1,0:T(8,128)S(1)} %copy.49.a_lo, f32[4,3,6,1536]{3,2,1,0:T(8,128)S(1)} %copy.50.a_hi, ...), custom_call_target="tpu_custom_call" | custom-call | flops 134217728 | bytes 1048576 | tf_op jit(solution)/shard_map/pallas_call | solution.py:273
  131.1 6.9 %shard_map.84.own_ref = f32[8,128]{1,0:T(8,128)} custom-call(f32[8,128]{1,0:T(8,128)} %copy-done.40), custom_call_target="tpu_custom_call" | custom-call | tf_op jit(solution)/shard_map/pallas_call | solution.py:237
  138.0 5.9 %shard_map.85 = f32[8,128]{1,0:T(8,128)} custom-call(f32[8,128]{1,0:T(8,128)} %shard_map.84.own_ref), custom_call_target="tpu_custom_call" | custom-call | tf_op jit(solution)/shard_map/pallas_call | solution.py:237
  147.4 2.0 copy-done.16
  155.0 3.5 %collective-permute-start.11 = (f32[4,6,3,1536]{3,0,2,1:T(4,128)S(1)}, f32[4,6,3,1536]{3,0,2,1:T(4,128)S(1)}, u32[]{:S(2)}, u32[]{:S(2)}) collective-permute-start(f32[4,6,3,1536]{3,0,2,1:T(4,128)S(1)} %copy.58), channel_id=1, source_target_pairs={{1,0},{2,1},{3,2},{4,3},{5,4},{6,5},{7,6},{0,7},{9,8},{10,9},{11,1... | collective-permute-start | bytes 1327112 | tf_op jit(solution)/shard_map/ppermute | solution.py:312
  159.8 2.6 %collective-permute-start.9 = (f32[4,3,6,1536]{3,0,2,1:T(4,128)S(1)}, f32[4,3,6,1536]{3,0,2,1:T(4,128)S(1)}, u32[]{:S(2)}, u32[]{:S(2)}) collective-permute-start(f32[4,3,6,1536]{3,0,2,1:T(4,128)S(1)} %copy.56), channel_id=1, source_target_pairs={{8,0},{16,8},{24,16},{0,24},{9,1},{17,9},{25,17},{1,25},{10,2},{18... | collective-permute-start | bytes 1327112 | tf_op jit(solution)/shard_map/ppermute | solution.py:312
  162.4 18.3 %shard_map.87 = (f32[4,6,6,1536]{3,2,1,0:T(8,128)S(1)}, f32[3,4,6,6,1536]{4,3,2,1,0:T(8,128)S(1)}, f32[3,6,1536]{2,1,0:T(8,128)S(1)}) custom-call(f32[5]{0:T(128)S(1)} %multiply.6.kappa_ref, f32[4,6,6,1536]{3,2,1,0:T(8,128)S(1)} %shard_map.86.v_ref, f32[6,6,1536]{2,1,0:T(8,128)S(1)} %copy-done.7, f32[4,6,384]{2,1,0:T(8,128)S(1)} %copy-done.31, ...), custom_call_target="tpu_custom_call" | custom-call | flops 268435456 | bytes 1048576 | tf_op jit(solution)/shard_map/pallas_call | solution.py:273
  180.7 1.7 copy-done.11
  183.7 10.4 %shard_map.88 = (f32[4,6,6,1536]{3,2,1,0:T(8,128)S(1)}, f32[2,4,6,6,1536]{4,3,2,1,0:T(8,128)S(1)}, f32[8,128]{1,0:T(8,128)S(1)}) custom-call(f32[5]{0:T(128)S(1)} %multiply.6.kappa_ref, f32[4,6,6,1536]{3,2,1,0:T(8,128)S(1)} %shard_map.86.v_ref, f32[4,3,6,1536]{3,2,1,0:T(8,128)S(1)} %copy.59.a_lo, f32[4,3,6,1536]{3,2,1,0:T(8,128)S(1)} %copy.60.a_hi, ...), custom_call_target="tpu_custom_call" | custom-call | flops 134217728 | bytes 1048576 | tf_op jit(solution)/shard_map/pallas_call | solution.py:273
  197.2 6.9 %shard_map.89.own_ref = f32[8,128]{1,0:T(8,128)} custom-call(f32[8,128]{1,0:T(8,128)} %copy-done.38), custom_call_target="tpu_custom_call" | custom-call | tf_op jit(solution)/shard_map/pallas_call | solution.py:237
  204.1 5.9 %shard_map.90 = f32[8,128]{1,0:T(8,128)} custom-call(f32[8,128]{1,0:T(8,128)} %shard_map.89.own_ref), custom_call_target="tpu_custom_call" | custom-call | tf_op jit(solution)/shard_map/pallas_call | solution.py:237
  212.8 2.0 copy-done.12
  (181 shorter events, 59.3 us)
Async XLA Ops:
  2.8 42.7 %collective-permute-start.1 = (f32[4,3,6,1536]{3,0,2,1:T(4,128)}, f32[4,3,6,1536]{3,0,2,1:T(4,128)}, u32[]{:S(2)}, u32[]{:S(2)}) collective-permute-start(f32[4,3,6,1536]{3,0,2,1:T(4,128)} %get-tuple-element.54), channel_id=1, source_target_pairs={{8,0},{16,8},{24,16},{0,24},{9,1},{17,9},{25,17},{1,25},{10,2},{18... | collective-permute-start | bytes 1327112 | tf_op jit(solution)/shard_map/ppermute | solution.py:312
  6.8 40.0 %collective-permute-start = (f32[4,3,6,1536]{3,0,2,1:T(4,128)}, f32[4,3,6,1536]{3,0,2,1:T(4,128)}, u32[]{:S(2)}, u32[]{:S(2)}) collective-permute-start(f32[4,3,6,1536]{3,0,2,1:T(4,128)} %get-tuple-element.55), channel_id=1, source_target_pairs={{0,8},{8,16},{16,24},{24,0},{1,9},{9,17},{17,25},{25,1},{2,10},{10... | collective-permute-start | bytes 1327112 | tf_op jit(solution)/shard_map/ppermute | solution.py:312
  7.8 40.1 %collective-permute-start.3 = (f32[4,6,3,1536]{3,0,2,1:T(4,128)}, f32[4,6,3,1536]{3,0,2,1:T(4,128)}, u32[]{:S(2)}, u32[]{:S(2)}) collective-permute-start(f32[4,6,3,1536]{3,0,2,1:T(4,128)} %get-tuple-element.52), channel_id=1, source_target_pairs={{1,0},{2,1},{3,2},{4,3},{5,4},{6,5},{7,6},{0,7},{9,8},{10,9},{11,1... | collective-permute-start | bytes 1327112 | tf_op jit(solution)/shard_map/ppermute | solution.py:312
  10.5 38.6 %collective-permute-start.2 = (f32[4,6,3,1536]{3,0,2,1:T(4,128)}, f32[4,6,3,1536]{3,0,2,1:T(4,128)}, u32[]{:S(2)}, u32[]{:S(2)}) collective-permute-start(f32[4,6,3,1536]{3,0,2,1:T(4,128)} %get-tuple-element.53), channel_id=1, source_target_pairs={{0,1},{1,2},{2,3},{3,4},{4,5},{5,6},{6,7},{7,0},{8,9},{9,10},{10,1... | collective-permute-start | bytes 1327112 | tf_op jit(solution)/shard_map/ppermute | solution.py:312
  13.7 36.7 %copy-start.3 = (f32[4,6,6,1536]{3,2,1,0:T(8,128)}, f32[4,6,6,1536]{3,2,1,0:T(8,128)S(1)}, u32[]{:S(2)}) copy-start(f32[4,6,6,1536]{3,2,1,0:T(8,128)S(1)} %copy.37.v_ref) | copy-start | bytes 2654212
  21.6 58.6 %copy-start = (s32[4,6,6,1536]{3,2,1,0:T(8,128)}, s32[4,6,6,1536]{3,2,1,0:T(8,128)S(1)}, u32[]{:S(2)}) copy-start(s32[4,6,6,1536]{3,2,1,0:T(8,128)S(1)} %copy.44.obstacle_ref) | copy-start | bytes 2654212
  23.1 27.3 %copy-start.32 = (f32[6,1,1536]{2,1,0:T(1,128)}, f32[6,1,1536]{2,1,0:T(1,128)S(1)}, u32[]{:S(2)}) copy-start(f32[6,1,1536]{2,1,0:T(1,128)S(1)} %multiply_multiply_fusion.2.f2_ref) | copy-start | bytes 110596
  23.1 21.6 %copy-start.48 = (f32[4]{0:T(128)S(1)}, f32[4]{0:T(128)}, u32[]{:S(2)}) copy-start(f32[4]{0:T(128)} %fusion.12) | copy-start | bytes 52
  23.9 22.8 %copy-start.5 = (f32[6,6,1536]{2,1,0:T(8,128)}, f32[6,6,1536]{2,1,0:T(8,128)S(1)}, u32[]{:S(2)}) copy-start(f32[6,6,1536]{2,1,0:T(8,128)S(1)} %multiply_multiply_fusion.1.f0_ref) | copy-start | bytes 663556
  24.6 22.1 %copy-start.8 = (f32[6,6,1536]{2,1,0:T(8,128)}, f32[6,6,1536]{2,1,0:T(8,128)S(1)}, u32[]{:S(2)}) copy-start(f32[6,6,1536]{2,1,0:T(8,128)S(1)} %multiply_multiply_fusion.f4_ref) | copy-start | bytes 663556
  24.7 22.0 %copy-start.29 = (f32[4,6,384]{2,1,0:T(8,128)}, f32[4,6,384]{2,1,0:T(8,128)S(1)}, u32[]{:S(2)}) copy-start(f32[4,6,384]{2,1,0:T(8,128)S(1)} %broadcast_in_dim.14.f3_ref) | copy-start | bytes 110596
  50.4 29.7 %copy-start.45 = (f32[5]{0:T(128)S(1)}, f32[5]{0:T(128)}, u32[]{:S(2)}) copy-start(f32[5]{0:T(128)} %constant.87) | copy-start | bytes 64
  89.1 27.3 %collective-permute-start.6 = (f32[4,6,3,1536]{3,0,2,1:T(4,128)S(1)}, f32[4,6,3,1536]{3,0,2,1:T(4,128)S(1)}, u32[]{:S(2)}, u32[]{:S(2)}) collective-permute-start(f32[4,6,3,1536]{3,0,2,1:T(4,128)S(1)} %copy.47), channel_id=1, source_target_pairs={{0,1},{1,2},{2,3},{3,4},{4,5},{5,6},{6,7},{7,0},{8,9},{9,10},{10,1... | collective-permute-start | bytes 1327112 | tf_op jit(solution)/shard_map/ppermute | solution.py:312
  89.1 27.4 %collective-permute-start.7 = (f32[4,6,3,1536]{3,0,2,1:T(4,128)S(1)}, f32[4,6,3,1536]{3,0,2,1:T(4,128)S(1)}, u32[]{:S(2)}, u32[]{:S(2)}) collective-permute-start(f32[4,6,3,1536]{3,0,2,1:T(4,128)S(1)} %copy.48), channel_id=1, source_target_pairs={{1,0},{2,1},{3,2},{4,3},{5,4},{6,5},{7,6},{0,7},{9,8},{10,9},{11,1... | collective-permute-start | bytes 1327112 | tf_op jit(solution)/shard_map/ppermute | solution.py:312
  92.9 23.9 %collective-permute-start.4 = (f32[4,3,6,1536]{3,0,2,1:T(4,128)S(1)}, f32[4,3,6,1536]{3,0,2,1:T(4,128)S(1)}, u32[]{:S(2)}, u32[]{:S(2)}) collective-permute-start(f32[4,3,6,1536]{3,0,2,1:T(4,128)S(1)} %copy.45), channel_id=1, source_target_pairs={{0,8},{8,16},{16,24},{24,0},{1,9},{9,17},{17,25},{25,1},{2,10},{10... | collective-permute-start | bytes 1327112 | tf_op jit(solution)/shard_map/ppermute | solution.py:312
  94.8 22.2 %collective-permute-start.5 = (f32[4,3,6,1536]{3,0,2,1:T(4,128)S(1)}, f32[4,3,6,1536]{3,0,2,1:T(4,128)S(1)}, u32[]{:S(2)}, u32[]{:S(2)}) collective-permute-start(f32[4,3,6,1536]{3,0,2,1:T(4,128)S(1)} %copy.46), channel_id=1, source_target_pairs={{8,0},{16,8},{24,16},{0,24},{9,1},{17,9},{25,17},{1,25},{10,2},{18... | collective-permute-start | bytes 1327112 | tf_op jit(solution)/shard_map/ppermute | solution.py:312
  117.6 27.2 %copy-start.46 = (f32[5]{0:T(128)S(1)}, f32[5]{0:T(128)}, u32[]{:S(2)}) copy-start(f32[5]{0:T(128)} %constant.81) | copy-start | bytes 64
  154.9 7.4 %copy-start.7 = (f32[6,6,1536]{2,1,0:T(8,128)S(1)}, f32[6,6,1536]{2,1,0:T(8,128)}, u32[]{:S(2)}) copy-start(f32[6,6,1536]{2,1,0:T(8,128)} %copy-done.5) | copy-start | bytes 663556
  155.0 27.4 %collective-permute-start.10 = (f32[4,6,3,1536]{3,0,2,1:T(4,128)S(1)}, f32[4,6,3,1536]{3,0,2,1:T(4,128)S(1)}, u32[]{:S(2)}, u32[]{:S(2)}) collective-permute-start(f32[4,6,3,1536]{3,0,2,1:T(4,128)S(1)} %copy.57), channel_id=1, source_target_pairs={{0,1},{1,2},{2,3},{3,4},{4,5},{5,6},{6,7},{7,0},{8,9},{9,10},{10,1... | collective-permute-start | bytes 1327112 | tf_op jit(solution)/shard_map/ppermute | solution.py:312
  155.0 27.6 %collective-permute-start.11 = (f32[4,6,3,1536]{3,0,2,1:T(4,128)S(1)}, f32[4,6,3,1536]{3,0,2,1:T(4,128)S(1)}, u32[]{:S(2)}, u32[]{:S(2)}) collective-permute-start(f32[4,6,3,1536]{3,0,2,1:T(4,128)S(1)} %copy.58), channel_id=1, source_target_pairs={{1,0},{2,1},{3,2},{4,3},{5,4},{6,5},{7,6},{0,7},{9,8},{10,9},{11,1... | collective-permute-start | bytes 1327112 | tf_op jit(solution)/shard_map/ppermute | solution.py:312
  158.9 24.1 %collective-permute-start.8 = (f32[4,3,6,1536]{3,0,2,1:T(4,128)S(1)}, f32[4,3,6,1536]{3,0,2,1:T(4,128)S(1)}, u32[]{:S(2)}, u32[]{:S(2)}) collective-permute-start(f32[4,3,6,1536]{3,0,2,1:T(4,128)S(1)} %copy.55), channel_id=1, source_target_pairs={{0,8},{8,16},{16,24},{24,0},{1,9},{9,17},{17,25},{25,1},{2,10},{10... | collective-permute-start | bytes 1327112 | tf_op jit(solution)/shard_map/ppermute | solution.py:312
  159.8 23.3 %collective-permute-start.9 = (f32[4,3,6,1536]{3,0,2,1:T(4,128)S(1)}, f32[4,3,6,1536]{3,0,2,1:T(4,128)S(1)}, u32[]{:S(2)}, u32[]{:S(2)}) collective-permute-start(f32[4,3,6,1536]{3,0,2,1:T(4,128)S(1)} %copy.56), channel_id=1, source_target_pairs={{8,0},{16,8},{24,16},{0,24},{9,1},{17,9},{25,17},{1,25},{10,2},{18... | collective-permute-start | bytes 1327112 | tf_op jit(solution)/shard_map/ppermute | solution.py:312
  183.7 27.1 %copy-start.47 = (f32[5]{0:T(128)S(1)}, f32[5]{0:T(128)}, u32[]{:S(2)}) copy-start(f32[5]{0:T(128)} %constant.81) | copy-start | bytes 64
  183.7 29.1 %copy-start.2 = (s32[4,6,6,1536]{3,2,1,0:T(8,128)S(1)}, s32[4,6,6,1536]{3,2,1,0:T(8,128)}, u32[]{:S(2)}) copy-start(s32[4,6,6,1536]{3,2,1,0:T(8,128)} %copy-done) | copy-start | bytes 2654212
  (41 other events, 109.8 us)
